TPU v7x, 256 devices: a whole 4x4x8 slice. The times are simulated.
256 devices in a mesh: dp: 2 (over core), glob: 4 (over y), byte: 32 (over z, x).
Axes of the slice: x: 4, y: 4, z: 8, core: 2. Of those that a mesh axis runs over, the one named last changes fastest.
Arguments:
- byte_states: bfloat16 [2, 4096, 4096], P('dp', 'byte', 'glob'), may hold values from -8 to 8
- patch_start: int32 [2, 32, 32], P('dp'), may hold values from 0 to 128, as said below
- queries: bfloat16 [2, 1024, 2048], P('dp', 'byte', 'glob'), may hold values from -6 to 6
- grad_out: bfloat16 [2, 1024, 2048], P('dp', 'byte', 'glob'), may hold values from -6 to 6
- w_kv: bfloat16 [2, 4096, 512], P(None, 'byte', 'glob'), may hold values from -0.09375 to 0.09375
Outputs:
- attended: bfloat16 [2, 1024, 2048], P('dp', 'byte', 'glob')
- grad_queries: bfloat16 [2, 1024, 2048], P('dp', 'byte', 'glob')
- grad_bytes: bfloat16 [2, 4096, 4096], P('dp', 'byte', 'glob')
- grad_kv: float32 [2, 4096, 512], P(None, 'byte', 'glob')
Inputs may be any that keep to these rules, and one draw needn't show every extreme that they name: Per shard: patch_start[s, 0] is 0, used slots come first with strictly rising starts, unused slots hold 128; a shard uses between 8 and 32 slots, and some shard of every draw uses all 32.
All inputs are finite; a program needn't handle non-finite values.
Results may differ from a plain program's by a relative error of at most 0.02.
Values may be sent and summed in bfloat16 or wider, within the bound.
No kernel may reach another device: no remote copies, remote signals or barrier semaphores. Data moves between devices by JAX's collectives and lax.ppermute only.
A program may use at most 64 MiB of HBM per device.

v0:
```python
import math

import jax
import jax.numpy as jnp
from jax import lax
from jax.sharding import Mesh
from jax.sharding import PartitionSpec as P

HS = 128
BYTE = ("byte_0", "byte_1")


def gather_axes(value, axes, dim):
    out = value
    for number in range(len(axes) - 1, -1, -1):
        out = lax.all_gather(out, axes[number], axis=dim, tiled=True)
    return out


def copy_for_each(value, axis):
    copies = jnp.broadcast_to(value, (lax.axis_size(axis), *value.shape))
    return lax.all_to_all(copies, axis, split_axis=0, concat_axis=0, tiled=True)


def joined_along(pieces, dim):
    shape = list(pieces.shape[1:])
    shape[dim] *= pieces.shape[0]
    return jnp.moveaxis(pieces, 0, dim).reshape(shape)


def gathered_copies(value, axis, dim):
    pieces = copy_for_each(value, axis)
    return joined_along(pieces, dim)


def sent_together(arrays, axis, dim, along):
    both = jnp.concatenate(arrays, axis=along)
    out, at, done = (lax.all_gather(both, axis, axis=dim, tiled=True), 0, [])
    for a in arrays:
        done.append(lax.slice_in_dim(out, at, at + a.shape[along], axis=along))
        at += a.shape[along]
    return tuple(done)


def split_up(value, dim, count):
    shape = value.shape
    pieces = value.reshape(*shape[:dim], count, shape[dim] // count, *shape[dim + 1 :])
    return jnp.moveaxis(pieces, dim, 0)


def summed_on_arrival(value, axis, dim):
    count = lax.axis_size(axis)
    pieces = lax.all_to_all(split_up(value, dim, count), axis, 0, 0, tiled=True)
    return jnp.sum(pieces.astype(jnp.float32), axis=0)


def sent_together_2(arrays, axis, dim, along):
    ends, at = ([], 0)
    for a in arrays[:-1]:
        at += a.shape[along]
        ends.append(at)
    both = jnp.concatenate(arrays, axis=along)
    return tuple(jnp.split(summed_on_arrival(both, axis, dim), ends, axis=along))


def taken_together(value, axis):
    everything = copy_for_each(value, axis)
    return jnp.sum(everything.astype(jnp.float32), axis=0)


def segment_of(offsets, length):
    position = jnp.arange(length, dtype=jnp.int32)
    opened = (offsets[:, None] <= position[None, :]).astype(jnp.int32)
    return jnp.sum(opened, axis=0) - 1


def contract_rows(left, right):
    return lax.dot_general(
        left, right, (((0,), (0,)), ((), ())), preferred_element_type=jnp.float32
    )


def contract_cols(left, right):
    return lax.dot_general(
        left, right, (((1,), (1,)), ((), ())), preferred_element_type=jnp.float32
    )


def on_device(byte_states, patch_start, queries, grad_out, w_kv):
    states = byte_states[0]
    all_offsets = patch_start[0]
    cotangent = grad_out[0]
    byte_count = states.shape[0]
    shard_total = all_offsets.shape[0]
    slot_count = all_offsets.shape[1]
    slot_total = shard_total * slot_count
    shard = lax.axis_index(BYTE)
    offsets = lax.dynamic_index_in_dim(all_offsets, shard, 0, keepdims=False)
    head_count = cotangent.shape[1] // HS
    shared_heads = w_kv.shape[2] // HS
    group_size = head_count // shared_heads
    factor = 1.0 / math.sqrt(HS)
    segments = segment_of(offsets, byte_count)
    slot_range = jnp.arange(slot_count, dtype=jnp.int32)
    members = slot_range[:, None] == segments[None, :]
    counts = jnp.maximum(jnp.sum(members.astype(jnp.float32), axis=1), 1.0)
    summed = jnp.dot(members.astype(jnp.bfloat16), states, preferred_element_type=jnp.float32)
    pooled_part = (summed / counts[:, None]).astype(jnp.bfloat16)
    usable = all_offsets.reshape(slot_total) < byte_count
    live = lax.dynamic_slice_in_dim(usable, shard * slot_count, slot_count, 0)
    pair_full = gather_axes(w_kv, BYTE, 1)
    pooled = gathered_copies(pooled_part, "glob", 1)
    key_rows = jnp.dot(pooled, pair_full[0], preferred_element_type=jnp.float32).astype(
        jnp.bfloat16
    )
    value_rows = jnp.dot(pooled, pair_full[1], preferred_element_type=jnp.float32).astype(
        jnp.bfloat16
    )
    key_all, value_all = sent_together((key_rows, value_rows), BYTE, 0, 1)
    block_len = math.gcd(slot_total, 1024)
    block_total = slot_total // block_len
    key_blocks = key_all.reshape(block_total, block_len, shared_heads, HS)
    value_blocks = value_all.reshape(block_total, block_len, shared_heads, HS)
    id_blocks = jnp.arange(slot_total, dtype=jnp.int32).reshape(block_total, block_len)
    usable_blocks = usable.reshape(block_total, block_len)
    query_heads = queries[0].reshape(slot_count, shared_heads, group_size, HS)
    query_ids = shard * slot_count + slot_range
    live_rows = live.astype(jnp.bfloat16)[:, None, None, None]
    masked_grad = cotangent.reshape(slot_count, shared_heads, group_size, HS) * live_rows

    def scores_of(key_block, id_block, usable_block):
        scores = (
            jnp.einsum("qcgd,kcd->cgqk", query_heads, key_block, preferred_element_type=jnp.float32)
            * factor
        )
        visible = (id_block[None, :] <= query_ids[:, None]) & usable_block[None, :]
        return (jnp.where(visible, scores, -1e30), visible)

    def first_pass(carried, blocks):
        highest, totals = carried
        key_block, id_block, usable_block = blocks
        masked, visible = scores_of(key_block, id_block, usable_block)
        newest = jnp.maximum(highest, jnp.max(masked, axis=-1))
        raised = jnp.where(visible, jnp.exp(masked - newest[..., None]), 0.0)
        totals = totals * jnp.exp(highest - newest) + jnp.sum(raised, axis=-1)
        return ((newest, totals), None)

    start_high = jnp.full((shared_heads, group_size, slot_count), -1e30, jnp.float32)
    (highest, totals), unused = lax.scan(
        first_pass, (start_high, jnp.zeros_like(start_high)), (key_blocks, id_blocks, usable_blocks)
    )
    totals = jnp.maximum(totals, 1.0)

    def attention_of(masked, visible):
        raised = jnp.where(visible, jnp.exp(masked - highest[..., None]), 0.0)
        return raised / totals[..., None]

    def second_pass(mixed, blocks):
        key_block, value_block, id_block, usable_block = blocks
        masked, visible = scores_of(key_block, id_block, usable_block)
        shortened = attention_of(masked, visible).astype(jnp.bfloat16)
        return (
            mixed
            + jnp.einsum(
                "cgqk,kcd->qcgd", shortened, value_block, preferred_element_type=jnp.float32
            ),
            None,
        )

    zero_heads = jnp.zeros((slot_count, shared_heads, group_size, HS), jnp.float32)
    all_blocks = (key_blocks, value_blocks, id_blocks, usable_blocks)
    mixed, unused = lax.scan(second_pass, zero_heads, all_blocks)
    attended = (mixed * live.astype(jnp.float32)[:, None, None, None]).astype(jnp.bfloat16)
    attended = attended.reshape(1, slot_count, head_count * HS)
    row_dots = jnp.einsum("qcgd,qcgd->cgq", masked_grad.astype(jnp.float32), mixed)

    def third_pass(query_acc, blocks):
        key_block, value_block, id_block, usable_block = blocks
        masked, visible = scores_of(key_block, id_block, usable_block)
        attention = attention_of(masked, visible)
        shortened = attention.astype(jnp.bfloat16)
        prob_grad = jnp.einsum(
            "qcgd,kcd->cgqk", masked_grad, value_block, preferred_element_type=jnp.float32
        )
        score_grad = (attention * (prob_grad - row_dots[..., None]) * factor).astype(jnp.bfloat16)
        query_acc = query_acc + jnp.einsum(
            "cgqk,kcd->qcgd", score_grad, key_block, preferred_element_type=jnp.float32
        )
        key_part = jnp.einsum(
            "cgqk,qcgd->kcd", score_grad, query_heads, preferred_element_type=jnp.float32
        )
        value_part = jnp.einsum(
            "cgqk,qcgd->kcd", shortened, masked_grad, preferred_element_type=jnp.float32
        )
        return (query_acc, (key_part, value_part))

    query_acc, (key_parts, value_parts) = lax.scan(third_pass, zero_heads, all_blocks)
    query_grad = query_acc.astype(jnp.bfloat16).reshape(1, slot_count, head_count * HS)
    key_terms = key_parts.reshape(slot_total, shared_heads * HS)
    value_terms = value_parts.reshape(slot_total, shared_heads * HS)
    key_sum, value_sum = sent_together_2(
        (key_terms.astype(jnp.bfloat16), value_terms.astype(jnp.bfloat16)), BYTE, 0, 1
    )
    key_grad = key_sum.astype(jnp.bfloat16)
    value_grad = value_sum.astype(jnp.bfloat16)
    patch_part = contract_cols(key_grad, pair_full[0]) + contract_cols(value_grad, pair_full[1])
    patch_grad = summed_on_arrival(patch_part.astype(jnp.bfloat16), "glob", 1).astype(jnp.bfloat16)
    pool_grad = patch_grad.astype(jnp.float32) / counts[:, None]
    byte_grad = jnp.take(pool_grad, segments, axis=0).astype(jnp.bfloat16)[None]
    key_value = jnp.concatenate([key_grad, value_grad], axis=1)
    pair_sum = summed_on_arrival(contract_rows(pooled, key_value).astype(jnp.bfloat16), BYTE, 0)
    pair_sum = taken_together(pair_sum.astype(jnp.bfloat16), "dp").astype(jnp.float32)
    pair_grad = pair_sum.reshape(pair_sum.shape[0], 2, shared_heads * HS).transpose(1, 0, 2)
    return (attended, query_grad, byte_grad, pair_grad)


def solution(mesh):
    torus = Mesh(
        mesh.devices.reshape(mesh.shape["dp"], mesh.shape["glob"], 8, 4),
        ("dp", "glob", "byte_0", "byte_1"),
    )
    in_specs = (
        P("dp", BYTE, "glob"),
        P("dp", None, None),
        P("dp", BYTE, "glob"),
        P("dp", BYTE, "glob"),
        P(None, BYTE, "glob"),
    )
    out_specs = (
        P("dp", BYTE, "glob"),
        P("dp", BYTE, "glob"),
        P("dp", BYTE, "glob"),
        P(None, BYTE, "glob"),
    )
    return jax.shard_map(
        on_device, mesh=torus, in_specs=in_specs, out_specs=out_specs, check_vma=False
    )
```

profile of v0, /device:TPU:1, one launch (start us, length us, event | category | flops | bytes accessed | tf_op | source)
XLA Modules:
  0.0 202.3 jit_solution(3882961190758477233)
XLA Ops:
  7.2 0.0 copy-start
  7.2 0.0 copy-start.5
  7.2 0.0 copy-start.4
  7.2 0.0 all-gather.2.cloned.1.call-start
  7.2 12.5 %all_gather.9 = bf16[2,512,128]{2,1,0:T(8,128)(2,1)} all-gather(bf16[2,128,128]{2,1,0:T(8,128)(2,1)} %param.9), channel_id=1, replica_groups=mesh['dp'=2,'glob'=4,'byte_0'=8,'byte_1'=4] {'byte_1'}, dimensions={1}, use_global_device_ids=true | all-gather | bytes 327680 | tf_op jit(solution)/shard_map/all_gather | solution.py:16
  19.8 0.0 all-gather.2.cloned.1.call-update
  19.8 0.7 dynamic-slice_bitcast_fusion
  20.5 0.1 convert_reduce_fusion.2
  20.6 0.1 convert_reduce_fusion.1
  20.7 0.0 copy-done
  20.7 0.2 fusion.11
  20.9 0.7 broadcast_in_dim.90
  21.6 4.2 %all-to-all-start = ((bf16[4,32,1024]{2,1,0:T(8,128)(2,1)}), bf16[4,32,1024]{2,1,0:T(8,128)(2,1)S(1)}, u32[]{:S(2)}, u32[]{:S(2)}) async-start(bf16[4,32,1024]{2,1,0:T(8,128)(2,1)} %broadcast_in_dim.90), calls=%async_computation | async-start | bytes 524288 | tf_op jit(solution)/shard_map/all_to_all | solution.py:22
  25.8 0.7 broadcast_compare_fusion
  26.5 0.1 lt.43
  26.6 0.0 copy-done.5
  26.7 0.0 copy-done.4
  26.7 0.1 dynamic-slice_convert_fusion
  26.8 0.1 broadcast_multiply_fusion
  26.9 0.1 fusion.23
  27.0 4.4 %all-to-all-done = bf16[4,32,1024]{2,1,0:T(8,128)(2,1)S(1)} async-done(((bf16[4,32,1024]{2,1,0:T(8,128)(2,1)}), bf16[4,32,1024]{2,1,0:T(8,128)(2,1)S(1)}, u32[]{:S(2)}, u32[]{:S(2)}) %all-to-all-start) | async-done | bytes 262176 | tf_op jit(solution)/shard_map/all_to_all | solution.py:22
  31.4 29.6 %all-gather.2.cloned.1.call-done = bf16[2,4096,128]{2,1,0:T(8,128)(2,1)} async-done(((bf16[2,512,128]{2,1,0:T(8,128)(2,1)}), bf16[2,4096,128]{2,1,0:T(8,128)(2,1)}) %all-gather.2.cloned.1.call-update) | async-done | bytes 2097168 | tf_op jit(solution)/shard_map/all_gather | solution.py:16
  61.0 1.5 convolution_convert_fusion.2
  62.5 1.5 convolution_convert_fusion.3
  64.0 37.1 %all_gather.11 = bf16[1024,256]{1,0:T(8,128)(2,1)S(1)} all-gather(bf16[32,256]{1,0:T(8,128)(2,1)S(1)} %pad_maximum_fusion.1), channel_id=1, replica_groups=mesh['dp'=2,'glob'=4,'byte_0'=8,'byte_1'=4] {'byte_0','byte_1'}, dimensions={0}, use_global_device_ids=true | all-gather | bytes 540672 | tf_op jit(solution)/shard_map/all_gather | solution.py:38
  101.1 0.0 copy-start.2
  101.1 0.3 fusion.36
  101.4 0.2 fusion.16
  101.7 0.3 fusion.25
  102.0 0.4 fusion.9
  102.4 0.2 fusion.24
  102.5 0.0 copy-done.2
  102.5 0.3 fusion.10
  102.8 0.0 copy-start.1
  102.8 1.0 fusion.6
  103.8 0.2 copy.39
  104.0 1.0 pad_maximum_fusion
  105.0 19.0 %all_to_all.25 = bf16[32,32,256]{2,1,0:T(8,128)(2,1)S(1)} all-to-all(bf16[32,32,256]{2,1,0:T(8,128)(2,1)S(1)} %pad_maximum_fusion), channel_id=1, replica_groups=mesh['dp'=2,'glob'=4,'byte_0'=8,'byte_1'=4] {'byte_0','byte_1'}, dimensions={0} | all-to-all | bytes 1048576 | tf_op jit(solution)/shard_map/all_to_all | solution.py:53
  124.0 0.1 reduce.4
  124.0 0.0 copy-done.1
  124.1 0.4 fusion.13
  124.5 0.5 fusion
  125.0 0.7 copy.65
  125.7 4.0 %all-to-all-start.2 = ((bf16[4,32,1024]{2,1,0:T(8,128)(2,1)}), bf16[4,32,1024]{2,1,0:T(8,128)(2,1)S(1)}, u32[]{:S(2)}, u32[]{:S(2)}) async-start(bf16[4,32,1024]{2,1,0:T(8,128)(2,1)} %bitcast.128), calls=%async_computation.2 | async-start | bytes 524288 | tf_op jit(solution)/shard_map/all_to_all | solution.py:53
  129.7 2.1 %convolution_convert_fusion = bf16[4096,256]{1,0:T(8,128)(2,1)} fusion(bf16[32,4096]{1,0:T(8,128)(2,1)S(1)} %bitcast.131, bf16[32,256]{1,0:T(8,128)(2,1)S(1)} %reduce.4), kind=kOutput, calls=%fused_computation.1 | convolution fusion | flops 68157440 | bytes 2375680 | tf_op jit(solution)/shard_map/dot_general | solution.py:78
  131.8 3.7 %all-to-all-done.2 = bf16[4,32,1024]{2,1,0:T(8,128)(2,1)S(1)} async-done(((bf16[4,32,1024]{2,1,0:T(8,128)(2,1)}), bf16[4,32,1024]{2,1,0:T(8,128)(2,1)S(1)}, u32[]{:S(2)}, u32[]{:S(2)}) %all-to-all-start.2) | async-done | bytes 262176 | tf_op jit(solution)/shard_map/all_to_all | solution.py:53
  135.5 0.0 copy-start.3
  135.5 4.1 %all-to-all-start.3 = ((bf16[32,128,256]{2,1,0:T(8,128)(2,1)}), bf16[32,128,256]{2,1,0:T(8,128)(2,1)S(1)}, u32[]{:S(2)}, u32[]{:S(2)}) async-start(bf16[32,128,256]{2,1,0:T(8,128)(2,1)} %bitcast.37), calls=%async_computation.3 | async-start | bytes 4194304 | tf_op jit(solution)/shard_map/all_to_all | solution.py:53
  139.7 0.6 reshape.201
  140.4 0.0 copy-done.3
  140.4 0.2 fusion.12
  140.6 0.6 reshape.204
  141.3 0.1 convert_divide_fusion
  141.4 0.9 gather_fusion
  142.3 0.8 fusion.14
  143.1 24.7 %all-to-all-done.3 = bf16[32,128,256]{2,1,0:T(8,128)(2,1)S(1)} async-done(((bf16[32,128,256]{2,1,0:T(8,128)(2,1)}), bf16[32,128,256]{2,1,0:T(8,128)(2,1)S(1)}, u32[]{:S(2)}, u32[]{:S(2)}) %all-to-all-start.3) | async-done | bytes 2097184 | tf_op jit(solution)/shard_map/all_to_all | solution.py:53
  167.8 0.3 reduce_sum.75
  168.1 26.4 %all_to_all.26 = bf16[2,128,256]{2,1,0:T(8,128)(2,1)S(1)} all-to-all(bf16[2,128,256]{2,1,0:T(8,128)(2,1)S(1)} %broadcast_in_dim.98), channel_id=1, replica_groups=mesh['dp'=2,'glob'=4,'byte_0'=8,'byte_1'=4] {'dp'}, dimensions={0} | all-to-all | bytes 262144 | tf_op jit(solution)/shard_map/all_to_all | solution.py:22
  194.6 0.1 copy.41
  194.7 0.8 copy.42
  (18 shorter events, 0.2 us)
Async XLA Ops:
  7.2 13.6 %copy-start = (bf16[1,128,1024]{2,1,0:T(8,128)(2,1)S(1)}, bf16[1,128,1024]{2,1,0:T(8,128)(2,1)}, u32[]{:S(2)}) copy-start(bf16[1,128,1024]{2,1,0:T(8,128)(2,1)} %param.5) | copy-start | bytes 786436
  7.2 19.5 %copy-start.5 = (bf16[1,32,512]{2,1,0:T(8,128)(2,1)S(1)}, bf16[1,32,512]{2,1,0:T(8,128)(2,1)}, u32[]{:S(2)}) copy-start(bf16[1,32,512]{2,1,0:T(8,128)(2,1)} %param.7) | copy-start | bytes 98308
  7.2 19.5 %copy-start.4 = (bf16[1,32,512]{2,1,0:T(8,128)(2,1)S(1)}, bf16[1,32,512]{2,1,0:T(8,128)(2,1)}, u32[]{:S(2)}) copy-start(bf16[1,32,512]{2,1,0:T(8,128)(2,1)} %param.8) | copy-start | bytes 98308
  7.2 53.8 %all-gather.2.cloned.1.call-start = ((), (), s32[]{:S(2)}) async-start(), calls=%async_computation.5 | async-start | bytes 2359296 | tf_op jit(solution)/shard_map/all_gather | solution.py:16
  21.6 9.7 %all-to-all-start = ((bf16[4,32,1024]{2,1,0:T(8,128)(2,1)}), bf16[4,32,1024]{2,1,0:T(8,128)(2,1)S(1)}, u32[]{:S(2)}, u32[]{:S(2)}) async-start(bf16[4,32,1024]{2,1,0:T(8,128)(2,1)} %broadcast_in_dim.90), calls=%async_computation | async-start | bytes 524288 | tf_op jit(solution)/shard_map/all_to_all | solution.py:22
  101.1 1.4 copy-start.2
  102.8 21.2 %copy-start.1 = (bf16[2,4096,128]{2,1,0:T(8,128)(2,1)S(1)}, bf16[2,4096,128]{2,1,0:T(8,128)(2,1)}, u32[]{:S(2)}) copy-start(bf16[2,4096,128]{2,1,0:T(8,128)(2,1)} %all-gather.2.cloned.1.call-done) | copy-start | bytes 6291460
  125.7 9.8 %all-to-all-start.2 = ((bf16[4,32,1024]{2,1,0:T(8,128)(2,1)}), bf16[4,32,1024]{2,1,0:T(8,128)(2,1)S(1)}, u32[]{:S(2)}, u32[]{:S(2)}) async-start(bf16[4,32,1024]{2,1,0:T(8,128)(2,1)} %bitcast.128), calls=%async_computation.2 | async-start | bytes 524288 | tf_op jit(solution)/shard_map/all_to_all | solution.py:53
  135.5 4.9 %copy-start.3 = (bf16[1024,256]{1,0:T(8,128)(2,1)S(1)}, bf16[1024,256]{1,0:T(8,128)(2,1)}, u32[]{:S(2)}) copy-start(bf16[1024,256]{1,0:T(8,128)(2,1)} %copy-done.2) | copy-start | bytes 1572868
  135.5 32.3 %all-to-all-start.3 = ((bf16[32,128,256]{2,1,0:T(8,128)(2,1)}), bf16[32,128,256]{2,1,0:T(8,128)(2,1)S(1)}, u32[]{:S(2)}, u32[]{:S(2)}) async-start(bf16[32,128,256]{2,1,0:T(8,128)(2,1)} %bitcast.37), calls=%async_computation.3 | async-start | bytes 4194304 | tf_op jit(solution)/shard_map/all_to_all | solution.py:53
Sparse Core Ops, SparseCore 0:
  19.9 41.0 all-gather.1
where the time goes:
time: 203 us; the launch traced here: 202 us
  blocking collectives  95 us (47%)
  waiting for transfers between devices  62.5 us (31%)
  between operations  14.3 us (7%)
  starting transfers between devices  12.4 us (6%)
  matrix products  8.63 us (4%)
  local copies, waits for them, and re-layouts  5.52 us (3%)
  other arithmetic  4.01 us (2%)
    all_gather x1, blocking collectives, sent_together(): out, at, done = (lax.all_gather(both, axis, axis=dim, tiled=True), 0, [])  37.1 us
    all_gather x1, waiting for transfers between devices, gather_axes(): out = lax.all_gather(out, axes[number], axis=dim, tiled=True)  29.6 us
    all_to_all x2, waiting for transfers between devices, summed_on_arrival(): pieces = lax.all_to_all(split_up(value, dim, count), axis, 0, 0, tiled=True)  28.5 us
    all_to_all x1, blocking collectives, copy_for_each(): return lax.all_to_all(copies, axis, split_axis=0, concat_axis=0, tiled=True)  26.4 us
    all_to_all x1, blocking collectives, summed_on_arrival(): pieces = lax.all_to_all(split_up(value, dim, count), axis, 0, 0, tiled=True)  19 us
    all_gather x1, blocking collectives, gather_axes(): out = lax.all_gather(out, axes[number], axis=dim, tiled=True)  12.5 us
    all_to_all x2, starting transfers between devices, summed_on_arrival(): pieces = lax.all_to_all(split_up(value, dim, count), axis, 0, 0, tiled=True)  8.14 us
    all_to_all x1, waiting for transfers between devices, copy_for_each(): return lax.all_to_all(copies, axis, split_axis=0, concat_axis=0, tiled=True)  4.37 us
  transfers between devices with their start and end apart: 4, of which 4 were waited for; matrix products, arithmetic and copies ran while one was open for 4% of the time, Pallas kernels for 0%

commit v1 on v0

--- a/solution.py
+++ b/solution.py
@@ -61,11 +61,6 @@
         ends.append(at)
     both = jnp.concatenate(arrays, axis=along)
     return tuple(jnp.split(summed_on_arrival(both, axis, dim), ends, axis=along))
-
-
-def taken_together(value, axis):
-    everything = copy_for_each(value, axis)
-    return jnp.sum(everything.astype(jnp.float32), axis=0)
 
 
 def segment_of(offsets, length):
@@ -108,7 +103,10 @@
     pooled_part = (summed / counts[:, None]).astype(jnp.bfloat16)
     usable = all_offsets.reshape(slot_total) < byte_count
     live = lax.dynamic_slice_in_dim(usable, shard * slot_count, slot_count, 0)
-    pair_full = gather_axes(w_kv, BYTE, 1)
+    core = lax.axis_index("dp")
+    own = lax.dynamic_index_in_dim(w_kv, core, 0, keepdims=False)
+    rows = copy_for_each(own, BYTE).reshape(-1, own.shape[1])
+    pair_full = copy_for_each(rows, "dp")
     pooled = gathered_copies(pooled_part, "glob", 1)
     key_rows = jnp.dot(pooled, pair_full[0], preferred_element_type=jnp.float32).astype(
         jnp.bfloat16
@@ -116,7 +114,9 @@
     value_rows = jnp.dot(pooled, pair_full[1], preferred_element_type=jnp.float32).astype(
         jnp.bfloat16
     )
-    key_all, value_all = sent_together((key_rows, value_rows), BYTE, 0, 1)
+    both_rows = jnp.concatenate([key_rows, value_rows], axis=1)
+    both_all = copy_for_each(both_rows, BYTE).reshape(slot_total, both_rows.shape[1])
+    key_all, value_all = jnp.split(both_all, 2, axis=1)
     block_len = math.gcd(slot_total, 1024)
     block_total = slot_total // block_len
     key_blocks = key_all.reshape(block_total, block_len, shared_heads, HS)
@@ -207,10 +207,10 @@
     patch_grad = summed_on_arrival(patch_part.astype(jnp.bfloat16), "glob", 1).astype(jnp.bfloat16)
     pool_grad = patch_grad.astype(jnp.float32) / counts[:, None]
     byte_grad = jnp.take(pool_grad, segments, axis=0).astype(jnp.bfloat16)[None]
-    key_value = jnp.concatenate([key_grad, value_grad], axis=1)
-    pair_sum = summed_on_arrival(contract_rows(pooled, key_value).astype(jnp.bfloat16), BYTE, 0)
-    pair_sum = taken_together(pair_sum.astype(jnp.bfloat16), "dp").astype(jnp.float32)
-    pair_grad = pair_sum.reshape(pair_sum.shape[0], 2, shared_heads * HS).transpose(1, 0, 2)
+    pair_part = jnp.stack([contract_rows(pooled, key_grad), contract_rows(pooled, value_grad)])
+    one_sum = summed_on_arrival(pair_part.astype(jnp.bfloat16), "dp", 0)[0]
+    one_sum = summed_on_arrival(one_sum.astype(jnp.bfloat16), BYTE, 0)
+    pair_grad = copy_for_each(one_sum, "dp")
     return (attended, query_grad, byte_grad, pair_grad)
 
 

time: 203 us -> 168 us (0.83)
  blocking collectives: 95 us -> 44.6 us
  starting transfers between devices: 12.4 us -> 29 us
  between operations: 14.3 us -> 0.97 us
  waiting for transfers between devices: 62.5 us -> 72.3 us
  local copies, waits for them, and re-layouts: 5.52 us -> 10.1 us
  matrix products: 8.63 us -> 6.07 us
    all_gather x2 -> x0, blocking collectives: 49.6 us -> none  [the longest x1 37.1 us: sent_together(): out, at, done = (lax.all_gather(both, axis, axis=dim, tiled=True), 0, [])]
    all_to_all x1 -> x3, waiting for transfers between devices: 4.37 us -> 45.6 us  [copy_for_each(): return lax.all_to_all(copies, axis, split_axis=0, concat_axis=0, tiled=True)]
    all_gather x1 -> x0, waiting for transfers between devices: 29.6 us -> none  [gather_axes(): out = lax.all_gather(out, axes[number], axis=dim, tiled=True)]
    all_to_all x1 -> x3, starting transfers between devices: 4.18 us -> 21.4 us  [copy_for_each(): return lax.all_to_all(copies, axis, split_axis=0, concat_axis=0, tiled=True)]
    all_to_all x1 -> x2, blocking collectives: 26.4 us -> 16 us  [copy_for_each(): return lax.all_to_all(copies, axis, split_axis=0, concat_axis=0, tiled=True)]
    all_to_all x1 -> x2, blocking collectives: 19 us -> 28.6 us  [summed_on_arrival(): pieces = lax.all_to_all(split_up(value, dim, count), axis, 0, 0, tiled=True)]
    broadcast_in_dim x2 -> x5, local copies, waits for them, and re-layouts: 0.74 us -> 2.95 us  [copy_for_each(): copies = jnp.broadcast_to(value, (lax.axis_size(axis), *value.shape))]
  transfers between devices with their start and end apart: 4 -> 5, of which waited for: 4 -> 5; matrix products, arithmetic and copies ran while one was open for 4% -> 4% of each run, Pallas kernels for 0% -> 0%
where the time goes in v1:
time: 168 us; the launch traced here: 167 us
  waiting for transfers between devices  72.3 us (43%)
  blocking collectives  44.6 us (27%)
  starting transfers between devices  29 us (17%)
  local copies, waits for them, and re-layouts  10.1 us (6%)
  matrix products  6.07 us (4%)
  other arithmetic  4.02 us (2%)
    all_to_all x3, waiting for transfers between devices, copy_for_each(): return lax.all_to_all(copies, axis, split_axis=0, concat_axis=0, tiled=True)  45.6 us
    all_to_all x2, blocking collectives, summed_on_arrival(): pieces = lax.all_to_all(split_up(value, dim, count), axis, 0, 0, tiled=True)  28.6 us
    all_to_all x2, waiting for transfers between devices, summed_on_arrival(): pieces = lax.all_to_all(split_up(value, dim, count), axis, 0, 0, tiled=True)  26.7 us
    all_to_all x3, starting transfers between devices, copy_for_each(): return lax.all_to_all(copies, axis, split_axis=0, concat_axis=0, tiled=True)  21.4 us
    all_to_all x2, blocking collectives, copy_for_each(): return lax.all_to_all(copies, axis, split_axis=0, concat_axis=0, tiled=True)  16 us
    all_to_all x2, starting transfers between devices, summed_on_arrival(): pieces = lax.all_to_all(split_up(value, dim, count), axis, 0, 0, tiled=True)  7.67 us
  transfers between devices with their start and end apart: 5, of which 5 were waited for; matrix products, arithmetic and copies ran while one was open for 4% of the time, Pallas kernels for 0%

profile of v1, /device:TPU:1, one launch (start us, length us, event | category | flops | bytes accessed | tf_op | source)
XLA Modules:
  0.0 167.2 jit_solution(629250969962319658)
XLA Ops:
  0.6 0.0 copy-start
  0.7 0.7 dynamic-slice_bitcast_fusion.1
  1.4 0.1 convert_reduce_fusion.2
  1.5 0.1 convert_reduce_fusion.1
  1.6 0.4 copy-done.9
  2.0 0.0 copy-done
  2.0 0.2 fusion.13
  2.2 0.7 broadcast_in_dim.99
  2.9 5.0 %all-to-all-start = ((bf16[4,32,1024]{2,1,0:T(8,128)(2,1)}), bf16[4,32,1024]{2,1,0:T(8,128)(2,1)S(1)}, u32[]{:S(2)}, u32[]{:S(2)}) async-start(bf16[4,32,1024]{2,1,0:T(8,128)(2,1)} %broadcast_in_dim.99), calls=%async_computation | async-start | bytes 524288 | tf_op jit(solution)/shard_map/all_to_all | solution.py:22
  7.9 0.8 dynamic-slice_bitcast_fusion
  8.7 4.8 %all-to-all-done = bf16[4,32,1024]{2,1,0:T(8,128)(2,1)S(1)} async-done(((bf16[4,32,1024]{2,1,0:T(8,128)(2,1)}), bf16[4,32,1024]{2,1,0:T(8,128)(2,1)S(1)}, u32[]{:S(2)}, u32[]{:S(2)}) %all-to-all-start) | async-done | bytes 262176 | tf_op jit(solution)/shard_map/all_to_all | solution.py:22
  13.4 1.2 broadcast_in_dim.100
  14.7 11.1 %all-to-all-start.1 = ((bf16[32,128,128]{2,1,0:T(8,128)(2,1)}), bf16[32,128,128]{2,1,0:T(8,128)(2,1)S(1)}, u32[]{:S(2)}, u32[]{:S(2)}) async-start(bf16[32,128,128]{2,1,0:T(8,128)(2,1)} %broadcast_in_dim.100), calls=%async_computation.1 | async-start | bytes 2097152 | tf_op jit(solution)/shard_map/all_to_all | solution.py:22
  25.8 24.7 %all-to-all-done.1 = bf16[32,128,128]{2,1,0:T(8,128)(2,1)S(1)} async-done(((bf16[32,128,128]{2,1,0:T(8,128)(2,1)}), bf16[32,128,128]{2,1,0:T(8,128)(2,1)S(1)}, u32[]{:S(2)}, u32[]{:S(2)}) %all-to-all-start.1) | async-done | bytes 1048608 | tf_op jit(solution)/shard_map/all_to_all | solution.py:22
  50.5 0.1 broadcast_in_dim.101
  50.6 9.3 %all_to_all.45 = bf16[2,4096,128]{2,1,0:T(8,128)(2,1)S(1)} all-to-all(bf16[2,4096,128]{2,1,0:T(8,128)(2,1)S(1)} %broadcast_in_dim.101), channel_id=1, replica_groups=mesh['dp'=2,'glob'=4,'byte_0'=8,'byte_1'=4] {'dp'}, dimensions={0} | all-to-all | bytes 4194304 | tf_op jit(solution)/shard_map/all_to_all | solution.py:22
  59.9 0.3 convolution_convert_fusion.3
  60.2 0.3 convolution_convert_fusion.4
  60.5 0.8 broadcast_in_dim.102
  61.4 5.3 %all-to-all-start.3 = ((bf16[32,32,256]{2,1,0:T(8,128)(2,1)}), bf16[32,32,256]{2,1,0:T(8,128)(2,1)S(1)}, u32[]{:S(2)}, u32[]{:S(2)}) async-start(bf16[32,32,256]{2,1,0:T(8,128)(2,1)} %broadcast_in_dim.102), calls=%async_computation.3 | async-start | bytes 1048576 | tf_op jit(solution)/shard_map/all_to_all | solution.py:22
  66.7 0.0 copy-done.8
  66.7 0.1 lt.48
  66.8 0.0 copy-done.7
  66.8 0.1 dynamic-slice_convert_fusion
  66.9 0.1 broadcast_multiply_fusion
  67.0 0.1 fusion.25
  67.1 16.2 %all-to-all-done.3 = bf16[32,32,256]{2,1,0:T(8,128)(2,1)S(1)} async-done(((bf16[32,32,256]{2,1,0:T(8,128)(2,1)}), bf16[32,32,256]{2,1,0:T(8,128)(2,1)S(1)}, u32[]{:S(2)}, u32[]{:S(2)}) %all-to-all-start.3) | async-done | bytes 524320 | tf_op jit(solution)/shard_map/all_to_all | solution.py:22
  83.3 0.3 fusion.40
  83.6 0.2 fusion.18
  83.9 0.3 fusion.27
  84.2 1.1 fusion.11
  85.3 0.2 fusion.26
  85.4 1.1 copy.37
  86.6 1.3 fusion.12
  87.9 0.0 copy-start.4
  87.9 0.3 fusion.8
  88.2 0.4 copy-done.4
  88.6 0.1 pad_maximum_fusion.1
  88.7 20.0 %all_to_all.46 = bf16[32,32,256]{2,1,0:T(8,128)(2,1)S(1)} all-to-all(bf16[32,32,256]{2,1,0:T(8,128)(2,1)S(1)} %pad_maximum_fusion.1), channel_id=1, replica_groups=mesh['dp'=2,'glob'=4,'byte_0'=8,'byte_1'=4] {'byte_0','byte_1'}, dimensions={0} | all-to-all | bytes 1048576 | tf_op jit(solution)/shard_map/all_to_all | solution.py:53
  108.6 0.1 reduce.5
  108.7 0.5 fusion.1
  109.2 0.5 fusion
  109.7 0.4 fusion.15
  110.1 0.5 fusion.2
  110.6 0.7 copy.61
  111.3 0.2 pad_maximum_fusion
  111.5 8.6 %all_to_all.47 = bf16[2,1,4096,128]{3,2,1,0:T(8,128)(2,1)S(1)} all-to-all(bf16[2,1,4096,128]{3,2,1,0:T(8,128)(2,1)S(1)} %pad_maximum_fusion), channel_id=1, replica_groups=mesh['dp'=2,'glob'=4,'byte_0'=8,'byte_1'=4] {'dp'}, dimensions={0} | all-to-all | bytes 4194304 | tf_op jit(solution)/shard_map/all_to_all | solution.py:53
  120.1 3.4 %all-to-all-start.5 = ((bf16[4,32,1024]{2,1,0:T(8,128)(2,1)}), bf16[4,32,1024]{2,1,0:T(8,128)(2,1)S(1)}, u32[]{:S(2)}, u32[]{:S(2)}) async-start(bf16[4,32,1024]{2,1,0:T(8,128)(2,1)} %bitcast.133), calls=%async_computation.5 | async-start | bytes 524288 | tf_op jit(solution)/shard_map/all_to_all | solution.py:53
  123.5 0.0 copy-start.10
  123.6 0.0 copy-start.5
  123.6 1.7 reduce_sum.75
  125.2 4.4 %all-to-all-done.5 = bf16[4,32,1024]{2,1,0:T(8,128)(2,1)S(1)} async-done(((bf16[4,32,1024]{2,1,0:T(8,128)(2,1)}), bf16[4,32,1024]{2,1,0:T(8,128)(2,1)S(1)}, u32[]{:S(2)}, u32[]{:S(2)}) %all-to-all-start.5) | async-done | bytes 262176 | tf_op jit(solution)/shard_map/all_to_all | solution.py:53
  129.6 4.3 %all-to-all-start.7 = ((bf16[32,128,128]{2,1,0:T(8,128)(2,1)}), bf16[32,128,128]{2,1,0:T(8,128)(2,1)S(1)}, u32[]{:S(2)}, u32[]{:S(2)}) async-start(bf16[32,128,128]{2,1,0:T(8,128)(2,1)} %bitcast.42), calls=%async_computation.7 | async-start | bytes 2097152 | tf_op jit(solution)/shard_map/all_to_all | solution.py:53
  134.0 0.6 reshape.242
  134.6 0.0 copy-done.2
  134.6 0.2 fusion.14
  134.9 0.6 reshape.245
  135.5 0.1 convert_divide_fusion
  135.6 0.9 gather_fusion
  136.5 0.8 fusion.16
  137.3 22.3 %all-to-all-done.7 = bf16[32,128,128]{2,1,0:T(8,128)(2,1)S(1)} async-done(((bf16[32,128,128]{2,1,0:T(8,128)(2,1)}), bf16[32,128,128]{2,1,0:T(8,128)(2,1)S(1)}, u32[]{:S(2)}, u32[]{:S(2)}) %all-to-all-start.7) | async-done | bytes 1048608 | tf_op jit(solution)/shard_map/all_to_all | solution.py:53
  159.6 0.2 convert_reduce_fusion
  159.8 6.7 %all_to_all.48 = f32[2,128,128]{2,1,0:T(8,128)S(1)} all-to-all(f32[2,128,128]{2,1,0:T(8,128)S(1)} %broadcast_in_dim.110), channel_id=1, replica_groups=mesh['dp'=2,'glob'=4,'byte_0'=8,'byte_1'=4] {'dp'}, dimensions={0} | all-to-all | bytes 262144 | tf_op jit(solution)/shard_map/all_to_all | solution.py:22
  166.5 0.7 copy.63
  (30 shorter events, 0.2 us)
Async XLA Ops:
  0.6 1.4 copy-start
  1.5 0.5 copy-start.9
  2.9 10.5 %all-to-all-start = ((bf16[4,32,1024]{2,1,0:T(8,128)(2,1)}), bf16[4,32,1024]{2,1,0:T(8,128)(2,1)S(1)}, u32[]{:S(2)}, u32[]{:S(2)}) async-start(bf16[4,32,1024]{2,1,0:T(8,128)(2,1)} %broadcast_in_dim.99), calls=%async_computation | async-start | bytes 524288 | tf_op jit(solution)/shard_map/all_to_all | solution.py:22
  14.7 35.8 %all-to-all-start.1 = ((bf16[32,128,128]{2,1,0:T(8,128)(2,1)}), bf16[32,128,128]{2,1,0:T(8,128)(2,1)S(1)}, u32[]{:S(2)}, u32[]{:S(2)}) async-start(bf16[32,128,128]{2,1,0:T(8,128)(2,1)} %broadcast_in_dim.100), calls=%async_computation.1 | async-start | bytes 2097152 | tf_op jit(solution)/shard_map/all_to_all | solution.py:22
  59.9 6.8 %copy-start.8 = (s32[1,32,32]{2,1,0:T(8,128)S(1)}, s32[1,32,32]{2,1,0:T(8,128)}, u32[]{:S(2)}) copy-start(s32[1,32,32]{2,1,0:T(8,128)} %param.6) | copy-start | bytes 12292
  59.9 6.9 %copy-start.7 = (bf16[1,32,512]{2,1,0:T(8,128)(2,1)S(1)}, bf16[1,32,512]{2,1,0:T(8,128)(2,1)}, u32[]{:S(2)}) copy-start(bf16[1,32,512]{2,1,0:T(8,128)(2,1)} %param.7) | copy-start | bytes 98308
  59.9 6.9 %copy-start.6 = (bf16[1,32,512]{2,1,0:T(8,128)(2,1)S(1)}, bf16[1,32,512]{2,1,0:T(8,128)(2,1)}, u32[]{:S(2)}) copy-start(bf16[1,32,512]{2,1,0:T(8,128)(2,1)} %param.8) | copy-start | bytes 98308
  61.4 21.9 %all-to-all-start.3 = ((bf16[32,32,256]{2,1,0:T(8,128)(2,1)}), bf16[32,32,256]{2,1,0:T(8,128)(2,1)S(1)}, u32[]{:S(2)}, u32[]{:S(2)}) async-start(bf16[32,32,256]{2,1,0:T(8,128)(2,1)} %broadcast_in_dim.102), calls=%async_computation.3 | async-start | bytes 1048576 | tf_op jit(solution)/shard_map/all_to_all | solution.py:22
  83.3 3.3 %copy-start.1 = (bf16[32,32,256]{2,1,0:T(8,128)(2,1)}, bf16[32,32,256]{2,1,0:T(8,128)(2,1)S(1)}, u32[]{:S(2)}) copy-start(bf16[32,32,256]{2,1,0:T(8,128)(2,1)S(1)} %all-to-all-done.3) | copy-start | bytes 1572868
  83.6 1.7 copy-start.3
  87.9 0.7 copy-start.4
  120.1 9.5 %all-to-all-start.5 = ((bf16[4,32,1024]{2,1,0:T(8,128)(2,1)}), bf16[4,32,1024]{2,1,0:T(8,128)(2,1)S(1)}, u32[]{:S(2)}, u32[]{:S(2)}) async-start(bf16[4,32,1024]{2,1,0:T(8,128)(2,1)} %bitcast.133), calls=%async_computation.5 | async-start | bytes 524288 | tf_op jit(solution)/shard_map/all_to_all | solution.py:53
  123.5 10.3 %copy-start.10 = (s32[128]{0:T(128)S(1)}, s32[128]{0:T(128)}, u32[]{:S(2)}) copy-start(s32[128]{0:T(128)} %copy-done.9) | copy-start | bytes 1540
  123.6 11.0 %copy-start.2 = (bf16[32,32,256]{2,1,0:T(8,128)(2,1)S(1)}, bf16[32,32,256]{2,1,0:T(8,128)(2,1)}, u32[]{:S(2)}) copy-start(bf16[32,32,256]{2,1,0:T(8,128)(2,1)} %copy-done.1) | copy-start | bytes 1572868
  123.6 11.0 %copy-start.5 = (bf16[4,32,1024]{2,1,0:T(8,128)(2,1)S(1)}, bf16[4,32,1024]{2,1,0:T(8,128)(2,1)}, u32[]{:S(2)}) copy-start(bf16[4,32,1024]{2,1,0:T(8,128)(2,1)} %copy-done.4) | copy-start | bytes 786436
  129.6 30.0 %all-to-all-start.7 = ((bf16[32,128,128]{2,1,0:T(8,128)(2,1)}), bf16[32,128,128]{2,1,0:T(8,128)(2,1)S(1)}, u32[]{:S(2)}, u32[]{:S(2)}) async-start(bf16[32,128,128]{2,1,0:T(8,128)(2,1)} %bitcast.42), calls=%async_computation.7 | async-start | bytes 2097152 | tf_op jit(solution)/shard_map/all_to_all | solution.py:53

commit v2 on v0

v2 whole, which is shorter than its diff:
```python
import functools
import math

import jax
import jax.numpy as jnp
from jax import lax
from jax.experimental import pallas as pl
from jax.experimental.pallas import tpu as pltpu
from jax.sharding import Mesh
from jax.sharding import PartitionSpec as P

HS = 128
BYTE = ("byte_0", "byte_1")
CROSS = ("glob", "byte_1")
BF = jnp.bfloat16
F32 = jnp.float32


def exchange(value, axes):
    return lax.all_to_all(value, axes, split_axis=0, concat_axis=0, tiled=True)


def dot(left, right, over):
    return lax.dot_general(left, right, ((over[0], over[1]), ((), ())), preferred_element_type=F32)


def rows_by_cols(left, right):
    return dot(left, right, ((1,), (0,)))


def rows_by_rows(left, right):
    return dot(left, right, ((1,), (1,)))


def cols_by_cols(left, right):
    return dot(left, right, ((0,), (0,)))


def call(body, outs, *operands, name):
    specs = [pl.BlockSpec(memory_space=pltpu.SMEM)]
    specs += [pl.BlockSpec(memory_space=pltpu.VMEM) for _ in operands[1:]]
    return pl.pallas_call(
        body,
        out_shape=outs,
        in_specs=specs,
        out_specs=jax.tree.map(lambda _: pl.BlockSpec(memory_space=pltpu.VMEM), outs),
        compiler_params=pltpu.CompilerParams(vmem_limit_bytes=16 * 2**20),
        name=name,
    )(*operands)


def shape(dims, dtype=BF):
    return jax.ShapeDtypeStruct(dims, dtype)


def members_of(starts_ref, shard, byte_count):
    slot_count = starts_ref.shape[1]
    row = starts_ref[pl.ds(shard, 1), :]
    position = lax.broadcasted_iota(jnp.int32, (byte_count, slot_count), 0)
    slot = lax.broadcasted_iota(jnp.int32, (byte_count, slot_count), 1)
    segment = jnp.sum((row <= position).astype(jnp.int32), axis=1, keepdims=True) - 1
    return (segment == slot).astype(F32).astype(BF)


def counts_of(members):
    ones = jnp.ones((members.shape[0], HS), BF)
    return jnp.maximum(cols_by_cols(members, ones), 1.0)[:, :1]


def pool_body(place_ref, starts_ref, states_ref, out_ref):
    members = members_of(starts_ref, place_ref[0], states_ref.shape[0])
    summed = cols_by_cols(members, states_ref[...])
    pooled = (summed / counts_of(members)).astype(BF)
    globs, xs = out_ref.shape[:2]
    halves = out_ref.shape[3] // HS
    for x in range(xs):
        for half in range(halves):
            at = (half * xs + x) * HS
            for y in range(globs):
                out_ref[y, x, :, half * HS : (half + 1) * HS] = pooled[:, at : at + HS]


def project_body(place_ref, pooled_ref, pair_ref, out_ref):
    globs, xs, slots, width = pooled_ref.shape
    copies = out_ref.shape[0]
    for which in range(2):
        total = None
        for y in range(globs):
            left = pooled_ref[y].reshape(xs * slots, width)
            for half in range(width // HS):
                part = rows_by_cols(
                    left[:, half * HS : (half + 1) * HS], pair_ref[y * (width // HS) + half, which]
                )
                total = part if total is None else total + part
        rounded = total.astype(BF)
        for copy in range(copies):
            out_ref[copy, :, which * HS : (which + 1) * HS] = rounded


def gathered_sum(ref):
    total = ref[0].astype(F32)
    for at in range(1, ref.shape[0]):
        total = total + ref[at].astype(F32)
    return total


def share_body(place_ref, parts_ref, out_ref):
    total = gathered_sum(parts_ref).astype(out_ref.dtype)
    for copy in range(out_ref.shape[0]):
        out_ref[copy] = total


def attend_body(
    place_ref, starts_ref, query_ref, grad_ref, both_ref, attended_ref, query_grad_ref, both_grad_ref,
    *, byte_count
):
    shard = place_ref[0]
    shard_total, slot_count = starts_ref.shape
    slot_total = shard_total * slot_count
    heads = query_ref.shape[1] // HS
    factor = 1.0 / math.sqrt(HS)
    used = jnp.sum((starts_ref[...] < byte_count).astype(jnp.int32), axis=1, keepdims=True)
    ids = lax.broadcasted_iota(jnp.int32, (shard_total, slot_total), 1)
    shards = lax.broadcasted_iota(jnp.int32, (shard_total, slot_total), 0)
    inside = ids - shards * slot_count
    usable = jnp.max(
        ((inside >= 0) & (inside < used)).astype(F32), axis=0, keepdims=True
    )
    mine = lax.broadcasted_iota(jnp.int32, (shard_total, 1), 0) == shard
    own_used = jnp.sum(jnp.where(mine, used, 0), axis=0, keepdims=True)
    live = (lax.broadcasted_iota(jnp.int32, (slot_count, 1), 0) < own_used).astype(F32)
    rows = lax.broadcasted_iota(jnp.int32, (slot_count, slot_total), 0) + shard * slot_count
    cols = lax.broadcasted_iota(jnp.int32, (slot_count, slot_total), 1)
    visible = (cols <= rows) & (usable > 0.0)
    keys = both_ref[:, :HS]
    values = both_ref[:, HS:]
    queries, grads, shorts, score_grads = [], [], [], []
    for head in range(heads):
        at = slice(head * HS, (head + 1) * HS)
        query = query_ref[:, at]
        grad = (grad_ref[:, at].astype(F32) * live).astype(BF)
        scores = jnp.where(visible, rows_by_rows(query, keys) * factor, -1e30)
        highest = jnp.max(scores, axis=1, keepdims=True)
        raised = jnp.where(visible, jnp.exp(scores - highest), 0.0)
        total = jnp.maximum(jnp.sum(raised, axis=1, keepdims=True), 1.0)
        attention = raised / total
        short = attention.astype(BF)
        mixed = rows_by_cols(short, values)
        attended_ref[:, at] = (mixed * live).astype(BF)
        dots = jnp.sum(grad.astype(F32) * mixed, axis=1, keepdims=True)
        prob_grad = rows_by_rows(grad, values)
        score_grad = (attention * (prob_grad - dots) * factor).astype(BF)
        query_grad_ref[:, at] = rows_by_cols(score_grad, keys).astype(BF)
        queries.append(query)
        grads.append(grad)
        shorts.append(short)
        score_grads.append(score_grad)
    queries = jnp.concatenate(queries, axis=0)
    grads = jnp.concatenate(grads, axis=0)
    both_grad_ref[:, :HS] = cols_by_cols(jnp.concatenate(score_grads, axis=0), queries).astype(BF)
    both_grad_ref[:, HS:] = cols_by_cols(jnp.concatenate(shorts, axis=0), grads).astype(BF)


def spread_body(place_ref, parts_ref, pooled_ref, pair_ref, patch_ref, weight_ref):
    both = gathered_sum(parts_ref).astype(BF)
    globs, xs, slots, width = pooled_ref.shape
    halves = width // HS
    for y in range(globs):
        left = pooled_ref[y].reshape(xs * slots, width)
        for half in range(halves):
            block = y * halves + half
            total = rows_by_rows(both[:, :HS], pair_ref[block, 0])
            total = total + rows_by_rows(both[:, HS:], pair_ref[block, 1])
            patch_ref[y, :, :, half * HS : (half + 1) * HS] = total.astype(BF).reshape(xs, slots, HS)
            grad = cols_by_cols(left[:, half * HS : (half + 1) * HS], both).astype(BF)
            weight_ref[0, block] = grad[:, :HS]
            weight_ref[1, block] = grad[:, HS:]


def byte_body(place_ref, starts_ref, parts_ref, out_ref):
    members = members_of(starts_ref, place_ref[0], out_ref.shape[0])
    counts = counts_of(members)
    globs, xs, slots, width = parts_ref.shape
    for x in range(xs):
        total = parts_ref[0, x].astype(F32)
        for y in range(1, globs):
            total = total + parts_ref[y, x].astype(F32)
        shared = (total.astype(BF).astype(F32) / counts).astype(BF)
        for half in range(width // HS):
            at = (half * xs + x) * HS
            out_ref[:, at : at + HS] = rows_by_cols(
                members, shared[:, half * HS : (half + 1) * HS]
            ).astype(BF)


def on_device(byte_states, patch_start, queries, grad_out, w_kv):
    states = byte_states[0]
    starts = patch_start[0]
    byte_count, width = states.shape
    shard_total, slot_count = starts.shape
    slot_total = shard_total * slot_count
    globs = lax.axis_size("glob")
    depth = lax.axis_size("byte_0")
    across = lax.axis_size("byte_1")
    block = slot_total // depth
    both = 2 * HS
    halves = width // (across * HS)
    place = jnp.reshape(lax.axis_index(BYTE), (1,)).astype(jnp.int32)

    pair = exchange(jnp.broadcast_to(w_kv, (depth, *w_kv.shape)), "byte_0")
    send = call(
        pool_body, shape((globs, across, slot_count, halves * HS)), place, starts, states, name="pool"
    )
    pooled = exchange(send.reshape(globs * across, slot_count, halves * HS), CROSS)
    pooled = pooled.reshape(globs, across, slot_count, halves * HS)
    send = call(project_body, shape((across, block, both)), place, pooled, pair, name="project")
    parts = exchange(send, "byte_1")
    send = call(share_body, shape((depth, block, both)), place, parts, name="share")
    key_value = exchange(send, "byte_0").reshape(slot_total, both)
    rows = queries.shape[1:]
    attended, query_grad, send = call(
        functools.partial(attend_body, byte_count=byte_count),
        (shape(rows), shape(rows), shape((slot_total, both))),
        place, starts, queries[0], grad_out[0], key_value,
        name="attend",
    )
    parts = exchange(send.reshape(depth, block, both), "byte_0")
    send = call(share_body, shape((across, block, both)), place, parts, name="share_grad")
    parts = exchange(send, "byte_1")
    patch_send, weight_send = call(
        spread_body,
        (shape((globs, across, slot_count, halves * HS)), shape((2, depth, HS, HS))),
        place, parts, pooled, pair,
        name="spread",
    )
    parts = exchange(patch_send.reshape(globs * across, slot_count, halves * HS), CROSS)
    parts = parts.reshape(globs, across, slot_count, halves * HS)
    weight_parts = exchange(weight_send, "dp")
    byte_grad = call(byte_body, shape((byte_count, width)), place, starts, parts, name="bytes")
    send = call(share_body, shape((1, depth, HS, HS)), place, weight_parts, name="sum_dp")
    weight_parts = exchange(send[0], "byte_0")
    send = call(share_body, shape((2, HS, HS), F32), place, weight_parts, name="sum_byte")
    pair_grad = exchange(send, "dp")
    return (attended[None], query_grad[None], byte_grad[None], pair_grad)


def solution(mesh):
    torus = Mesh(
        mesh.devices.reshape(mesh.shape["dp"], mesh.shape["glob"], 8, 4),
        ("dp", "glob", "byte_0", "byte_1"),
    )
    in_specs = (
        P("dp", BYTE, "glob"),
        P("dp", None, None),
        P("dp", BYTE, "glob"),
        P("dp", BYTE, "glob"),
        P(None, BYTE, "glob"),
    )
    out_specs = (
        P("dp", BYTE, "glob"),
        P("dp", BYTE, "glob"),
        P("dp", BYTE, "glob"),
        P(None, BYTE, "glob"),
    )
    return jax.shard_map(
        on_device, mesh=torus, in_specs=in_specs, out_specs=out_specs, check_vma=False
    )
```

time: 203 us -> 137 us (0.67)
  waiting for transfers between devices: 62.5 us -> 16.2 us
  between operations: 14.3 us -> 0.73 us
  matrix products: 8.63 us -> 0 us
  Pallas kernels: 0 us -> 7.63 us
  blocking collectives: 95 us -> 102 us
  starting transfers between devices: 12.4 us -> 7.56 us
  other arithmetic: 4.01 us -> 0 us
  local copies, waits for them, and re-layouts: 5.52 us -> 2.42 us
    all_to_all x2 -> x8, blocking collectives: 45.4 us -> 102 us  [exchange(): return lax.all_to_all(value, axes, split_axis=0, concat_axis=0, tiled=True)]
    all_gather x2 -> x0, blocking collectives: 49.6 us -> none  [the longest x1 37.1 us: sent_together(): out, at, done = (lax.all_gather(both, axis, axis=dim, tiled=True), 0, [])]
    all_gather x1 -> x0, waiting for transfers between devices: 29.6 us -> none  [gather_axes(): out = lax.all_gather(out, axes[number], axis=dim, tiled=True)]
    all_to_all x3 -> x2, waiting for transfers between devices: 32.8 us -> 16.2 us  [exchange(): return lax.all_to_all(value, axes, split_axis=0, concat_axis=0, tiled=True)]
    dot_general x12 -> x0, matrix products: 8.63 us -> none  [the longest x1 2.11 us: contract_rows(): lax.dot_general(left, right, (((0,), (0,)), ((), ())), preferred_element_...]
    pallas_call x0 -> x9, Pallas kernels: none -> 7.63 us  [call(): pl.pallas_call(body, out_shape=outs, in_specs=specs, out_specs=jax.tree.m...]
    all_to_all x3 -> x2, starting transfers between devices: 12.3 us -> 7.56 us  [exchange(): return lax.all_to_all(value, axes, split_axis=0, concat_axis=0, tiled=True)]
  transfers between devices with their start and end apart: 4 -> 2, of which waited for: 4 -> 2; matrix products, arithmetic and copies ran while one was open for 4% -> 0% of each run, Pallas kernels for 0% -> 2%
where the time goes in v2:
time: 137 us; the launch traced here: 136 us
  blocking collectives  102 us (74%)
  waiting for transfers between devices  16.2 us (12%)
  Pallas kernels  7.63 us (6%)
  starting transfers between devices  7.56 us (6%)
  local copies, waits for them, and re-layouts  2.42 us (2%)
    all_to_all x8, blocking collectives, exchange(): return lax.all_to_all(value, axes, split_axis=0, concat_axis=0, tiled=True)  102 us
    all_to_all x2, waiting for transfers between devices, exchange(): return lax.all_to_all(value, axes, split_axis=0, concat_axis=0, tiled=True)  16.2 us
    pallas_call x9, Pallas kernels, call(): pl.pallas_call(body, out_shape=outs, in_specs=specs, out_specs=jax.tree.m...  7.63 us
    all_to_all x2, starting transfers between devices, exchange(): return lax.all_to_all(value, axes, split_axis=0, concat_axis=0, tiled=True)  7.56 us
  transfers between devices with their start and end apart: 2, of which 2 were waited for; matrix products, arithmetic and copies ran while one was open for 0% of the time, Pallas kernels for 2%

profile of v2, /device:TPU:1, one launch (start us, length us, event | category | flops | bytes accessed | tf_op | source)
XLA Modules:
  0.0 136.2 jit_solution(12907791052770200173)
XLA Ops:
  0.6 0.0 copy-start.1
  0.6 0.7 copy-done.1
  1.3 0.0 copy-start
  1.4 0.9 copy-done
  2.3 0.4 pool.1
  2.8 0.0 copy-start.4
  2.8 15.1 %all_to_all.50 = bf16[16,32,256]{2,1,0:T(8,128)(2,1)S(1)} all-to-all(bf16[16,32,256]{2,1,0:T(8,128)(2,1)S(1)} %bitcast.19), channel_id=1, replica_groups=mesh['dp'=2,'glob'=4,'byte_0'=8,'byte_1'=4] {'glob','byte_1'}, dimensions={0} | all-to-all | bytes 524288 | tf_op jit(solution)/shard_map/all_to_all | solution.py:20
  17.8 0.0 copy-done.4
  17.8 0.1 broadcast_in_dim.12
  17.9 22.5 %all_to_all.51.pair_ref = bf16[8,2,128,128]{3,2,1,0:T(8,128)(2,1)S(1)} all-to-all(bf16[8,2,128,128]{3,2,1,0:T(8,128)(2,1)S(1)} %broadcast_in_dim.12), channel_id=1, replica_groups=mesh['dp'=2,'glob'=4,'byte_0'=8,'byte_1'=4] {'byte_0'}, dimensions={0} | all-to-all | bytes 1048576 | tf_op jit(solution)/shard_map/all_to_all | solution.py:20
  40.4 0.3 project.1
  40.7 7.9 %all_to_all.52.parts_ref = bf16[4,128,256]{2,1,0:T(8,128)(2,1)S(1)} all-to-all(bf16[4,128,256]{2,1,0:T(8,128)(2,1)S(1)} %project.1), channel_id=1, replica_groups=mesh['dp'=2,'glob'=4,'byte_0'=8,'byte_1'=4] {'byte_1'}, dimensions={0} | all-to-all | bytes 524288 | tf_op jit(solution)/shard_map/all_to_all | solution.py:20
  48.7 0.0 copy-start.2
  48.7 0.0 copy-start.3
  48.7 16.1 %all_to_all.53 = bf16[8,128,256]{2,1,0:T(8,128)(2,1)S(1)} all-to-all(bf16[8,128,256]{2,1,0:T(8,128)(2,1)S(1)} %share.1), channel_id=1, replica_groups=mesh['dp'=2,'glob'=4,'byte_0'=8,'byte_1'=4] {'byte_0'}, dimensions={0} | all-to-all | bytes 1048576 | tf_op jit(solution)/shard_map/all_to_all | solution.py:20
  64.8 0.0 copy-done.2
  64.8 0.0 copy-done.3
  64.8 3.4 %attend.1 = (bf16[32,512]{1,0:T(8,128)(2,1)}, bf16[32,512]{1,0:T(8,128)(2,1)}, bf16[1024,256]{1,0:T(8,128)(2,1)S(1)}) custom-call(s32[1]{0:T(128)} %bitcast.place_ref, s32[32,32]{1,0:T(8,128)S(1)} %bitcast.23, bf16[32,512]{1,0:T(8,128)(2,1)S(1)} %bitcast.25, bf16[32,512]{1,0:T(8,128)(2,1)S(1)} %bitcast.26, bf16[1024,256]{1,0:T(8,128)(2,1)S(1)} %bitcast.17), custom_call_target="tpu_custom_call" | custom-call | tf_op jit(solution)/shard_map/attend/pallas_call | solution.py:42
  68.2 14.7 %all_to_all.54.parts_ref = bf16[8,128,256]{2,1,0:T(8,128)(2,1)S(1)} all-to-all(bf16[8,128,256]{2,1,0:T(8,128)(2,1)S(1)} %bitcast.20), channel_id=1, replica_groups=mesh['dp'=2,'glob'=4,'byte_0'=8,'byte_1'=4] {'byte_0'}, dimensions={0} | all-to-all | bytes 1048576 | tf_op jit(solution)/shard_map/all_to_all | solution.py:20
  82.9 0.1 share_grad.1
  82.9 7.9 %all_to_all.55.parts_ref = bf16[4,128,256]{2,1,0:T(8,128)(2,1)S(1)} all-to-all(bf16[4,128,256]{2,1,0:T(8,128)(2,1)S(1)} %share_grad.1), channel_id=1, replica_groups=mesh['dp'=2,'glob'=4,'byte_0'=8,'byte_1'=4] {'byte_1'}, dimensions={0} | all-to-all | bytes 524288 | tf_op jit(solution)/shard_map/all_to_all | solution.py:20
  90.9 1.3 spread.1
  92.1 11.4 %all_to_all.56.parts_ref = bf16[2,8,128,128]{3,2,1,0:T(8,128)(2,1)S(1)} all-to-all(bf16[2,8,128,128]{3,2,1,0:T(8,128)(2,1)S(1)} %get-tuple-element.13), channel_id=1, replica_groups=mesh['dp'=2,'glob'=4,'byte_0'=8,'byte_1'=4] {'dp'}, dimensions={0} | all-to-all | bytes 1048576 | tf_op jit(solution)/shard_map/all_to_all | solution.py:20
  103.5 4.1 %all-to-all-start.6 = ((bf16[16,32,256]{2,1,0:T(8,128)(2,1)}), bf16[16,32,256]{2,1,0:T(8,128)(2,1)S(1)}, u32[]{:S(2)}, u32[]{:S(2)}) async-start(bf16[16,32,256]{2,1,0:T(8,128)(2,1)} %bitcast.11), calls=%async_computation.6 | async-start | bytes 524288 | tf_op jit(solution)/shard_map/all_to_all | solution.py:20
  107.7 0.8 sum_dp.1
  108.5 7.3 %all-to-all-done.6 = bf16[16,32,256]{2,1,0:T(8,128)(2,1)S(1)} async-done(((bf16[16,32,256]{2,1,0:T(8,128)(2,1)}), bf16[16,32,256]{2,1,0:T(8,128)(2,1)S(1)}, u32[]{:S(2)}, u32[]{:S(2)}) %all-to-all-start.6) | async-done | bytes 262176 | tf_op jit(solution)/shard_map/all_to_all | solution.py:20
  115.8 3.4 %all-to-all-start.8 = ((bf16[8,128,128]{2,1,0:T(8,128)(2,1)}), bf16[8,128,128]{2,1,0:T(8,128)(2,1)S(1)}, u32[]{:S(2)}, u32[]{:S(2)}) async-start(bf16[8,128,128]{2,1,0:T(8,128)(2,1)} %bitcast.14), calls=%async_computation.8 | async-start | bytes 524288 | tf_op jit(solution)/shard_map/all_to_all | solution.py:20
  119.2 1.3 bytes.1
  120.5 8.8 %all-to-all-done.8.parts_ref = bf16[8,128,128]{2,1,0:T(8,128)(2,1)S(1)} async-done(((bf16[8,128,128]{2,1,0:T(8,128)(2,1)}), bf16[8,128,128]{2,1,0:T(8,128)(2,1)S(1)}, u32[]{:S(2)}, u32[]{:S(2)}) %all-to-all-start.8) | async-done | bytes 262176 | tf_op jit(solution)/shard_map/all_to_all | solution.py:20
  129.4 6.1 %all_to_all.57 = f32[2,128,128]{2,1,0:T(8,128)S(1)} all-to-all(f32[2,128,128]{2,1,0:T(8,128)S(1)} %sum_byte.1), channel_id=1, replica_groups=mesh['dp'=2,'glob'=4,'byte_0'=8,'byte_1'=4] {'dp'}, dimensions={0} | all-to-all | bytes 262144 | tf_op jit(solution)/shard_map/all_to_all | solution.py:20
  135.5 0.7 copy.10
  (2 shorter events, 0.1 us)
Async XLA Ops:
  0.6 0.7 copy-start.1
  1.3 0.9 copy-start
  2.8 15.1 %copy-start.4 = (bf16[2,128,128]{2,1,0:T(8,128)(2,1)S(1)}, bf16[2,128,128]{2,1,0:T(8,128)(2,1)}, u32[]{:S(2)}) copy-start(bf16[2,128,128]{2,1,0:T(8,128)(2,1)} %param.9) | copy-start | bytes 196612
  48.7 16.1 %copy-start.2 = (bf16[1,32,512]{2,1,0:T(8,128)(2,1)S(1)}, bf16[1,32,512]{2,1,0:T(8,128)(2,1)}, u32[]{:S(2)}) copy-start(bf16[1,32,512]{2,1,0:T(8,128)(2,1)} %param.7) | copy-start | bytes 98308
  48.7 16.1 %copy-start.3 = (bf16[1,32,512]{2,1,0:T(8,128)(2,1)S(1)}, bf16[1,32,512]{2,1,0:T(8,128)(2,1)}, u32[]{:S(2)}) copy-start(bf16[1,32,512]{2,1,0:T(8,128)(2,1)} %param.8) | copy-start | bytes 98308
  103.5 12.3 %all-to-all-start.6 = ((bf16[16,32,256]{2,1,0:T(8,128)(2,1)}), bf16[16,32,256]{2,1,0:T(8,128)(2,1)S(1)}, u32[]{:S(2)}, u32[]{:S(2)}) async-start(bf16[16,32,256]{2,1,0:T(8,128)(2,1)} %bitcast.11), calls=%async_computation.6 | async-start | bytes 524288 | tf_op jit(solution)/shard_map/all_to_all | solution.py:20
  115.8 13.5 %all-to-all-start.8 = ((bf16[8,128,128]{2,1,0:T(8,128)(2,1)}), bf16[8,128,128]{2,1,0:T(8,128)(2,1)S(1)}, u32[]{:S(2)}, u32[]{:S(2)}) async-start(bf16[8,128,128]{2,1,0:T(8,128)(2,1)} %bitcast.14), calls=%async_computation.8 | async-start | bytes 524288 | tf_op jit(solution)/shard_map/all_to_all | solution.py:20

commit v3 on v2

--- a/solution.py
+++ b/solution.py
@@ -11,7 +11,8 @@
 
 HS = 128
 BYTE = ("byte_0", "byte_1")
-CROSS = ("glob", "byte_1")
+CROSS = ("dp", "glob", "byte_1")
+NEAR = ("dp", "byte_1")
 BF = jnp.bfloat16
 F32 = jnp.float32
 
@@ -67,34 +68,57 @@
     return jnp.maximum(cols_by_cols(members, ones), 1.0)[:, :1]
 
 
+def first_half(shape):
+    return lax.broadcasted_iota(jnp.int32, shape, 1) < HS // 2
+
+
+def halves_paired(low, high, first):
+    select = first_half(low.shape)
+    if first:
+        return jnp.where(select, low, pltpu.roll(high, HS // 2, 1))
+    return jnp.where(select, pltpu.roll(low, HS // 2, 1), high)
+
+
 def pool_body(place_ref, starts_ref, states_ref, out_ref):
     members = members_of(starts_ref, place_ref[0], states_ref.shape[0])
     summed = cols_by_cols(members, states_ref[...])
-    pooled = (summed / counts_of(members)).astype(BF)
-    globs, xs = out_ref.shape[:2]
-    halves = out_ref.shape[3] // HS
+    pooled = summed / counts_of(members)
+    cores, globs, xs = out_ref.shape[:3]
     for x in range(xs):
-        for half in range(halves):
-            at = (half * xs + x) * HS
+        low = pooled[:, x * HS : (x + 1) * HS]
+        high = pooled[:, (xs + x) * HS : (xs + x + 1) * HS]
+        for core in range(cores):
+            piece = halves_paired(low, high, core == 0).astype(BF)
             for y in range(globs):
-                out_ref[y, x, :, half * HS : (half + 1) * HS] = pooled[:, at : at + HS]
+                out_ref[core, y, x] = piece
+
+
+def copy_body(place_ref, pair_ref, out_ref):
+    depth, rows = out_ref.shape[:2]
+    at = pl.multiple_of(place_ref[1] * rows, rows)
+    for which in range(2):
+        piece = pair_ref[which, pl.ds(at, rows), :]
+        for z in range(depth):
+            out_ref[z, :, which * HS : (which + 1) * HS] = piece
+
+
+def features_of(pooled_ref, core):
+    globs, xs, slots = pooled_ref.shape[1:4]
+    pieces = [pooled_ref[core, y].reshape(xs * slots, HS) for y in range(globs)]
+    return jnp.concatenate(pieces, axis=1)
+
+
+def weights_of(pair_ref):
+    depth, rows, cols = pair_ref.shape
+    return pair_ref[...].reshape(depth * rows, cols)
 
 
 def project_body(place_ref, pooled_ref, pair_ref, out_ref):
-    globs, xs, slots, width = pooled_ref.shape
-    copies = out_ref.shape[0]
-    for which in range(2):
-        total = None
-        for y in range(globs):
-            left = pooled_ref[y].reshape(xs * slots, width)
-            for half in range(width // HS):
-                part = rows_by_cols(
-                    left[:, half * HS : (half + 1) * HS], pair_ref[y * (width // HS) + half, which]
-                )
-                total = part if total is None else total + part
-        rounded = total.astype(BF)
-        for copy in range(copies):
-            out_ref[copy, :, which * HS : (which + 1) * HS] = rounded
+    weights = weights_of(pair_ref)
+    for core in range(out_ref.shape[0]):
+        rounded = rows_by_cols(features_of(pooled_ref, core), weights).astype(BF)
+        for copy in range(out_ref.shape[1]):
+            out_ref[core, copy] = rounded
 
 
 def gathered_sum(ref):
@@ -162,35 +186,45 @@
 
 
 def spread_body(place_ref, parts_ref, pooled_ref, pair_ref, patch_ref, weight_ref):
-    both = gathered_sum(parts_ref).astype(BF)
-    globs, xs, slots, width = pooled_ref.shape
-    halves = width // HS
-    for y in range(globs):
-        left = pooled_ref[y].reshape(xs * slots, width)
-        for half in range(halves):
-            block = y * halves + half
-            total = rows_by_rows(both[:, :HS], pair_ref[block, 0])
-            total = total + rows_by_rows(both[:, HS:], pair_ref[block, 1])
-            patch_ref[y, :, :, half * HS : (half + 1) * HS] = total.astype(BF).reshape(xs, slots, HS)
-            grad = cols_by_cols(left[:, half * HS : (half + 1) * HS], both).astype(BF)
-            weight_ref[0, block] = grad[:, :HS]
-            weight_ref[1, block] = grad[:, HS:]
+    weights = weights_of(pair_ref)
+    cores, globs, xs, slots = pooled_ref.shape[:4]
+    grads = []
+    for core in range(cores):
+        total = parts_ref[core * xs].astype(F32)
+        for x in range(1, xs):
+            total = total + parts_ref[core * xs + x].astype(F32)
+        grad = total.astype(BF)
+        patch = rows_by_rows(grad, weights).astype(BF)
+        for y in range(globs):
+            patch_ref[core, y] = patch[:, y * HS : (y + 1) * HS].reshape(xs, slots, HS)
+        grads.append(grad)
+    features = jnp.concatenate([features_of(pooled_ref, core) for core in range(cores)], axis=0)
+    weight = cols_by_cols(features, jnp.concatenate(grads, axis=0)).astype(BF)
+    weight_ref[...] = weight.reshape(weight_ref.shape)
 
 
 def byte_body(place_ref, starts_ref, parts_ref, out_ref):
     members = members_of(starts_ref, place_ref[0], out_ref.shape[0])
     counts = counts_of(members)
-    globs, xs, slots, width = parts_ref.shape
+    cores, globs, xs = parts_ref.shape[:3]
     for x in range(xs):
-        total = parts_ref[0, x].astype(F32)
-        for y in range(1, globs):
-            total = total + parts_ref[y, x].astype(F32)
-        shared = (total.astype(BF).astype(F32) / counts).astype(BF)
-        for half in range(width // HS):
+        totals = []
+        for core in range(cores):
+            total = parts_ref[core, 0, x].astype(F32)
+            for y in range(1, globs):
+                total = total + parts_ref[core, y, x].astype(F32)
+            totals.append(total.astype(BF).astype(F32) / counts)
+        for half in range(2):
+            shared = halves_paired(*totals, half == 0).astype(BF)
             at = (half * xs + x) * HS
-            out_ref[:, at : at + HS] = rows_by_cols(
-                members, shared[:, half * HS : (half + 1) * HS]
-            ).astype(BF)
+            out_ref[:, at : at + HS] = rows_by_cols(members, shared).astype(BF)
+
+
+def total_body(place_ref, parts_ref, out_ref):
+    total = gathered_sum(parts_ref)
+    for copy in range(out_ref.shape[0]):
+        for which in range(2):
+            out_ref[copy, which] = total[:, which * HS : (which + 1) * HS]
 
 
 def on_device(byte_states, patch_start, queries, grad_out, w_kv):
@@ -199,22 +233,22 @@
     byte_count, width = states.shape
     shard_total, slot_count = starts.shape
     slot_total = shard_total * slot_count
+    cores = lax.axis_size("dp")
     globs = lax.axis_size("glob")
     depth = lax.axis_size("byte_0")
     across = lax.axis_size("byte_1")
     block = slot_total // depth
     both = 2 * HS
-    halves = width // (across * HS)
-    place = jnp.reshape(lax.axis_index(BYTE), (1,)).astype(jnp.int32)
-
-    pair = exchange(jnp.broadcast_to(w_kv, (depth, *w_kv.shape)), "byte_0")
-    send = call(
-        pool_body, shape((globs, across, slot_count, halves * HS)), place, starts, states, name="pool"
-    )
-    pooled = exchange(send.reshape(globs * across, slot_count, halves * HS), CROSS)
-    pooled = pooled.reshape(globs, across, slot_count, halves * HS)
-    send = call(project_body, shape((across, block, both)), place, pooled, pair, name="project")
-    parts = exchange(send, "byte_1")
+    half = HS // cores
+    pieces = (cores, globs, across, slot_count, HS)
+    place = jnp.stack([lax.axis_index(BYTE), lax.axis_index("dp")]).astype(jnp.int32)
+
+    send = call(copy_body, shape((depth, half, both)), place, w_kv, name="copies")
+    pair = exchange(send, "byte_0")
+    send = call(pool_body, shape(pieces), place, starts, states, name="pool")
+    pooled = exchange(send.reshape(-1, slot_count, HS), CROSS).reshape(pieces)
+    send = call(project_body, shape((cores, across, block, both)), place, pooled, pair, name="project")
+    parts = exchange(send.reshape(-1, block, both), NEAR)
     send = call(share_body, shape((depth, block, both)), place, parts, name="share")
     key_value = exchange(send, "byte_0").reshape(slot_total, both)
     rows = queries.shape[1:]
@@ -225,22 +259,17 @@
         name="attend",
     )
     parts = exchange(send.reshape(depth, block, both), "byte_0")
-    send = call(share_body, shape((across, block, both)), place, parts, name="share_grad")
-    parts = exchange(send, "byte_1")
+    send = call(share_body, shape((cores * across, block, both)), place, parts, name="share_grad")
+    parts = exchange(send, NEAR)
     patch_send, weight_send = call(
-        spread_body,
-        (shape((globs, across, slot_count, halves * HS)), shape((2, depth, HS, HS))),
-        place, parts, pooled, pair,
+        spread_body, (shape(pieces), shape((depth, half, both))), place, parts, pooled, pair,
         name="spread",
     )
-    parts = exchange(patch_send.reshape(globs * across, slot_count, halves * HS), CROSS)
-    parts = parts.reshape(globs, across, slot_count, halves * HS)
-    weight_parts = exchange(weight_send, "dp")
+    parts = exchange(patch_send.reshape(-1, slot_count, HS), CROSS).reshape(pieces)
     byte_grad = call(byte_body, shape((byte_count, width)), place, starts, parts, name="bytes")
-    send = call(share_body, shape((1, depth, HS, HS)), place, weight_parts, name="sum_dp")
-    weight_parts = exchange(send[0], "byte_0")
-    send = call(share_body, shape((2, HS, HS), F32), place, weight_parts, name="sum_byte")
-    pair_grad = exchange(send, "dp")
+    weight_parts = exchange(weight_send, "byte_0")
+    send = call(total_body, shape((cores, 2, half, HS), F32), place, weight_parts, name="total")
+    pair_grad = exchange(send, "dp").transpose(1, 0, 2, 3).reshape(w_kv.shape)
     return (attended[None], query_grad[None], byte_grad[None], pair_grad)
 
 

time: 137 us -> 149 us (1.088)
  Pallas kernels: 7.63 us -> 12.4 us
  starting transfers between devices: 7.56 us -> 12.1 us
  blocking collectives: 102 us -> 104 us
    pallas_call x9, Pallas kernels: 7.63 us -> 12.4 us  [call(): pl.pallas_call(body, out_shape=outs, in_specs=specs, out_specs=jax.tree.m...]
    all_to_all x2, starting transfers between devices: 7.56 us -> 12.1 us  [exchange(): return lax.all_to_all(value, axes, split_axis=0, concat_axis=0, tiled=True)]
    all_to_all x8 -> x7, blocking collectives: 102 us -> 104 us  [exchange(): return lax.all_to_all(value, axes, split_axis=0, concat_axis=0, tiled=True)]
where the time goes in v3:
time: 149 us; the launch traced here: 148 us
  blocking collectives  104 us (70%)
  waiting for transfers between devices  16.2 us (11%)
  Pallas kernels  12.4 us (8%)
  starting transfers between devices  12.1 us (8%)
  local copies, waits for them, and re-layouts  2.26 us (2%)
    all_to_all x7, blocking collectives, exchange(): return lax.all_to_all(value, axes, split_axis=0, concat_axis=0, tiled=True)  104 us
    all_to_all x2, waiting for transfers between devices, exchange(): return lax.all_to_all(value, axes, split_axis=0, concat_axis=0, tiled=True)  16.2 us
    pallas_call x9, Pallas kernels, call(): pl.pallas_call(body, out_shape=outs, in_specs=specs, out_specs=jax.tree.m...  12.4 us
    all_to_all x2, starting transfers between devices, exchange(): return lax.all_to_all(value, axes, split_axis=0, concat_axis=0, tiled=True)  12.1 us
  transfers between devices with their start and end apart: 2, of which 2 were waited for; matrix products, arithmetic and copies ran while one was open for 0% of the time, Pallas kernels for 2%

profile of v3, /device:TPU:1, one launch (start us, length us, event | category | flops | bytes accessed | tf_op | source)
XLA Modules:
  0.0 148.0 jit_solution(13825735253157065536)
XLA Ops:
  0.6 0.0 copy-start.1
  0.6 0.1 pad_add_fusion.place_ref
  0.7 0.6 copy-done.1
  1.3 0.0 copy-start
  1.4 0.9 copy-done
  2.3 1.8 %pool.1 = bf16[2,4,4,32,128]{4,3,2,1,0:T(8,128)(2,1)} custom-call(s32[2]{0:T(128)S(1)} %pad_add_fusion.place_ref, s32[32,32]{1,0:T(8,128)S(1)} %bitcast.26, bf16[128,1024]{1,0:T(8,128)(2,1)S(1)} %bitcast.24), custom_call_target="tpu_custom_call" | custom-call | tf_op jit(solution)/shard_map/pool/pallas_call | solution.py:43
  4.1 0.0 copy-start.2
  4.1 8.7 %all-to-all-start = ((bf16[32,32,128]{2,1,0:T(8,128)(2,1)}), bf16[32,32,128]{2,1,0:T(8,128)(2,1)S(1)}, u32[]{:S(2)}, u32[]{:S(2)}) async-start(bf16[32,32,128]{2,1,0:T(8,128)(2,1)} %bitcast.6), calls=%async_computation | async-start | bytes 524288 | tf_op jit(solution)/shard_map/all_to_all | solution.py:21
  12.8 0.0 copy-done.2
  12.8 0.6 copies.1
  13.4 7.7 %all-to-all-done = bf16[32,32,128]{2,1,0:T(8,128)(2,1)S(1)} async-done(((bf16[32,32,128]{2,1,0:T(8,128)(2,1)}), bf16[32,32,128]{2,1,0:T(8,128)(2,1)S(1)}, u32[]{:S(2)}, u32[]{:S(2)}) %all-to-all-start) | async-done | bytes 262176 | tf_op jit(solution)/shard_map/all_to_all | solution.py:21
  21.1 18.2 %all_to_all.45.pair_ref = bf16[8,64,256]{2,1,0:T(8,128)(2,1)S(1)} all-to-all(bf16[8,64,256]{2,1,0:T(8,128)(2,1)S(1)} %copies.1), channel_id=1, replica_groups=mesh['dp'=2,'glob'=4,'byte_0'=8,'byte_1'=4] {'byte_0'}, dimensions={0} | all-to-all | bytes 524288 | tf_op jit(solution)/shard_map/all_to_all | solution.py:21
  39.3 0.8 project.1
  40.1 15.0 %all_to_all.46.parts_ref = bf16[8,128,256]{2,1,0:T(8,128)(2,1)S(1)} all-to-all(bf16[8,128,256]{2,1,0:T(8,128)(2,1)S(1)} %bitcast.21), channel_id=1, replica_groups=mesh['dp'=2,'glob'=4,'byte_0'=8,'byte_1'=4] {'dp','byte_1'}, dimensions={0} | all-to-all | bytes 1048576 | tf_op jit(solution)/shard_map/all_to_all | solution.py:21
  55.1 0.6 share.1
  55.7 0.0 copy-start.3
  55.7 0.0 copy-start.4
  55.7 20.4 %all_to_all.47 = bf16[8,128,256]{2,1,0:T(8,128)(2,1)S(1)} all-to-all(bf16[8,128,256]{2,1,0:T(8,128)(2,1)S(1)} %share.1), channel_id=1, replica_groups=mesh['dp'=2,'glob'=4,'byte_0'=8,'byte_1'=4] {'byte_0'}, dimensions={0} | all-to-all | bytes 1048576 | tf_op jit(solution)/shard_map/all_to_all | solution.py:21
  76.1 0.0 copy-done.3
  76.1 0.0 copy-done.4
  76.1 3.9 %attend.1 = (bf16[32,512]{1,0:T(8,128)(2,1)}, bf16[32,512]{1,0:T(8,128)(2,1)}, bf16[1024,256]{1,0:T(8,128)(2,1)S(1)}) custom-call(s32[2]{0:T(128)S(1)} %pad_add_fusion.place_ref, s32[32,32]{1,0:T(8,128)S(1)} %bitcast.27, bf16[32,512]{1,0:T(8,128)(2,1)S(1)} %bitcast.29, bf16[32,512]{1,0:T(8,128)(2,1)S(1)} %bitcast.30, bf16[1024,256]{1,0:T(8,128)(2,1)S(1)} %bitcast.20), custom_call_target="tpu_custom_call" | custom-call | tf_op jit(solution)/shard_map/attend/pallas_call | solution.py:43
  80.0 20.2 %all_to_all.48.parts_ref = bf16[8,128,256]{2,1,0:T(8,128)(2,1)S(1)} all-to-all(bf16[8,128,256]{2,1,0:T(8,128)(2,1)S(1)} %bitcast.23), channel_id=1, replica_groups=mesh['dp'=2,'glob'=4,'byte_0'=8,'byte_1'=4] {'byte_0'}, dimensions={0} | all-to-all | bytes 1048576 | tf_op jit(solution)/shard_map/all_to_all | solution.py:21
  100.3 0.6 share_grad.1
  100.9 12.4 %all_to_all.49.parts_ref = bf16[8,128,256]{2,1,0:T(8,128)(2,1)S(1)} all-to-all(bf16[8,128,256]{2,1,0:T(8,128)(2,1)S(1)} %share_grad.1), channel_id=1, replica_groups=mesh['dp'=2,'glob'=4,'byte_0'=8,'byte_1'=4] {'dp','byte_1'}, dimensions={0} | all-to-all | bytes 1048576 | tf_op jit(solution)/shard_map/all_to_all | solution.py:21
  113.2 1.6 %spread.1 = (bf16[2,4,4,32,128]{4,3,2,1,0:T(8,128)(2,1)S(1)}, bf16[8,64,256]{2,1,0:T(8,128)(2,1)}) custom-call(s32[2]{0:T(128)S(1)} %pad_add_fusion.place_ref, bf16[8,128,256]{2,1,0:T(8,128)(2,1)S(1)} %all_to_all.49.parts_ref, bf16[2,4,4,32,128]{4,3,2,1,0:T(8,128)(2,1)S(1)} %bitcast.19, bf16[8,64,256]{2,1,0:T(8,128)(2,1)S(1)} %all_to_all.45.pair_ref), custom_call_target="tpu_custom_call" | custom-call | tf_op jit(solution)/shard_map/spread/pallas_call | solution.py:43
  114.9 12.2 %all_to_all.50 = bf16[32,32,128]{2,1,0:T(8,128)(2,1)S(1)} all-to-all(bf16[32,32,128]{2,1,0:T(8,128)(2,1)S(1)} %bitcast.25), channel_id=1, replica_groups=mesh['dp'=2,'glob'=4,'byte_0'=8,'byte_1'=4] {'dp','glob','byte_1'}, dimensions={0} | all-to-all | bytes 524288 | tf_op jit(solution)/shard_map/all_to_all | solution.py:21
  127.1 3.4 %all-to-all-start.7 = ((bf16[8,64,256]{2,1,0:T(8,128)(2,1)}), bf16[8,64,256]{2,1,0:T(8,128)(2,1)S(1)}, u32[]{:S(2)}, u32[]{:S(2)}) async-start(bf16[8,64,256]{2,1,0:T(8,128)(2,1)} %get-tuple-element.13), calls=%async_computation.7 | async-start | bytes 524288 | tf_op jit(solution)/shard_map/all_to_all | solution.py:21
  130.5 1.9 %bytes.1 = bf16[128,1024]{1,0:T(8,128)(2,1)} custom-call(s32[2]{0:T(128)S(1)} %pad_add_fusion.place_ref, s32[32,32]{1,0:T(8,128)S(1)} %bitcast.28, bf16[2,4,4,32,128]{4,3,2,1,0:T(8,128)(2,1)S(1)} %bitcast.22), custom_call_target="tpu_custom_call" | custom-call | tf_op jit(solution)/shard_map/bytes/pallas_call | solution.py:43
  132.4 8.4 %all-to-all-done.7.parts_ref = bf16[8,64,256]{2,1,0:T(8,128)(2,1)S(1)} async-done(((bf16[8,64,256]{2,1,0:T(8,128)(2,1)}), bf16[8,64,256]{2,1,0:T(8,128)(2,1)S(1)}, u32[]{:S(2)}, u32[]{:S(2)}) %all-to-all-start.7) | async-done | bytes 262176 | tf_op jit(solution)/shard_map/all_to_all | solution.py:21
  140.8 0.6 total.1
  141.4 5.9 %all_to_all.51 = f32[2,2,64,128]{3,2,1,0:T(8,128)S(1)} all-to-all(f32[2,2,64,128]{3,2,1,0:T(8,128)S(1)} %total.1), channel_id=1, replica_groups=mesh['dp'=2,'glob'=4,'byte_0'=8,'byte_1'=4] {'dp'}, dimensions={0} | all-to-all | bytes 262144 | tf_op jit(solution)/shard_map/all_to_all | solution.py:21
  147.3 0.7 copy.9
Async XLA Ops:
  0.6 0.7 copy-start.1
  1.3 0.9 copy-start
  4.1 8.7 %copy-start.2 = (bf16[2,128,128]{2,1,0:T(8,128)(2,1)S(1)}, bf16[2,128,128]{2,1,0:T(8,128)(2,1)}, u32[]{:S(2)}) copy-start(bf16[2,128,128]{2,1,0:T(8,128)(2,1)} %pair_ref.1) | copy-start | bytes 196612
  4.1 17.1 %all-to-all-start = ((bf16[32,32,128]{2,1,0:T(8,128)(2,1)}), bf16[32,32,128]{2,1,0:T(8,128)(2,1)S(1)}, u32[]{:S(2)}, u32[]{:S(2)}) async-start(bf16[32,32,128]{2,1,0:T(8,128)(2,1)} %bitcast.6), calls=%async_computation | async-start | bytes 524288 | tf_op jit(solution)/shard_map/all_to_all | solution.py:21
  55.7 20.4 %copy-start.3 = (bf16[1,32,512]{2,1,0:T(8,128)(2,1)S(1)}, bf16[1,32,512]{2,1,0:T(8,128)(2,1)}, u32[]{:S(2)}) copy-start(bf16[1,32,512]{2,1,0:T(8,128)(2,1)} %param.7) | copy-start | bytes 98308
  55.7 20.4 %copy-start.4 = (bf16[1,32,512]{2,1,0:T(8,128)(2,1)S(1)}, bf16[1,32,512]{2,1,0:T(8,128)(2,1)}, u32[]{:S(2)}) copy-start(bf16[1,32,512]{2,1,0:T(8,128)(2,1)} %param.8) | copy-start | bytes 98308
  127.1 13.7 %all-to-all-start.7 = ((bf16[8,64,256]{2,1,0:T(8,128)(2,1)}), bf16[8,64,256]{2,1,0:T(8,128)(2,1)S(1)}, u32[]{:S(2)}, u32[]{:S(2)}) async-start(bf16[8,64,256]{2,1,0:T(8,128)(2,1)} %get-tuple-element.13), calls=%async_computation.7 | async-start | bytes 524288 | tf_op jit(solution)/shard_map/all_to_all | solution.py:21

commit v4 on v2

v4 whole, which is shorter than its diff:
```python
import functools
import math

import jax
import jax.numpy as jnp
from jax import lax
from jax.experimental import pallas as pl
from jax.experimental.pallas import tpu as pltpu
from jax.sharding import Mesh
from jax.sharding import PartitionSpec as P

HS = 128
BYTE = ("byte_0", "byte_1")
CROSS = ("glob", "byte_1")
BF = jnp.bfloat16
F32 = jnp.float32


def exchange(value, axes):
    return lax.all_to_all(value, axes, split_axis=0, concat_axis=0, tiled=True)


def dot(left, right, over):
    return lax.dot_general(left, right, ((over[0], over[1]), ((), ())), preferred_element_type=F32)


def rows_by_cols(left, right):
    return dot(left, right, ((1,), (0,)))


def rows_by_rows(left, right):
    return dot(left, right, ((1,), (1,)))


def cols_by_cols(left, right):
    return dot(left, right, ((0,), (0,)))


def call(body, outs, *operands, name):
    specs = [pl.BlockSpec(memory_space=pltpu.VMEM) for _ in operands]
    return pl.pallas_call(
        body,
        out_shape=outs,
        in_specs=specs,
        out_specs=jax.tree.map(lambda _: pl.BlockSpec(memory_space=pltpu.VMEM), outs),
        compiler_params=pltpu.CompilerParams(vmem_limit_bytes=16 * 2**20),
        name=name,
    )(*operands)


def shape(dims, dtype=BF):
    return jax.ShapeDtypeStruct(dims, dtype)


def members_of(starts_ref, shard, byte_count):
    slot_count = starts_ref.shape[1]
    row = starts_ref[pl.ds(shard, 1), :]
    position = lax.broadcasted_iota(jnp.int32, (byte_count, slot_count), 0)
    slot = lax.broadcasted_iota(jnp.int32, (byte_count, slot_count), 1)
    segment = jnp.sum((row <= position).astype(jnp.int32), axis=1, keepdims=True) - 1
    return (segment == slot).astype(F32).astype(BF)


def counts_of(members):
    ones = jnp.ones((members.shape[0], HS), BF)
    return jnp.maximum(cols_by_cols(members, ones), 1.0)[:, :1]


def pool_body(starts_ref, states_ref, out_ref):
    members = members_of(starts_ref, lax.axis_index(BYTE), states_ref.shape[0])
    summed = cols_by_cols(members, states_ref[...])
    pooled = (summed / counts_of(members)).astype(BF)
    globs, xs = out_ref.shape[:2]
    halves = out_ref.shape[3] // HS
    for x in range(xs):
        for half in range(halves):
            at = (half * xs + x) * HS
            for y in range(globs):
                out_ref[y, x, :, half * HS : (half + 1) * HS] = pooled[:, at : at + HS]


def copy_body(pair_ref, out_ref):
    first = lax.axis_index("dp") == 0
    piece = jnp.where(first, pair_ref[0], pair_ref[1])
    for z in range(out_ref.shape[0]):
        out_ref[z] = piece


def features_of(pooled_ref):
    globs, xs, slots, width = pooled_ref.shape
    return jnp.concatenate([pooled_ref[y].reshape(xs * slots, width) for y in range(globs)], axis=1)


def pair_of(own_ref, other_ref):
    flat = (own_ref.shape[0] * own_ref.shape[1], own_ref.shape[2])
    return own_ref[...].reshape(flat), other_ref[...].reshape(flat)


def ordered(own, other):
    first = lax.axis_index("dp") == 0
    return jnp.where(first, own, other), jnp.where(first, other, own)


def project_body(pooled_ref, own_ref, other_ref, out_ref):
    left = features_of(pooled_ref)
    parts = [rows_by_cols(left, m).astype(BF) for m in ordered(*pair_of(own_ref, other_ref))]
    for copy in range(out_ref.shape[0]):
        for which in range(2):
            out_ref[copy, :, which * HS : (which + 1) * HS] = parts[which]


def gathered_sum(ref):
    total = ref[0].astype(F32)
    for at in range(1, ref.shape[0]):
        total = total + ref[at].astype(F32)
    return total


def share_body(parts_ref, out_ref):
    total = gathered_sum(parts_ref).astype(out_ref.dtype)
    for copy in range(out_ref.shape[0]):
        out_ref[copy] = total


def stacked(value, heads):
    return jnp.concatenate([value[:, h * HS : (h + 1) * HS] for h in range(heads)], axis=0)


def side_by_side(value, heads):
    rows = value.shape[0] // heads
    return jnp.concatenate([value[h * rows : (h + 1) * rows] for h in range(heads)], axis=1)


def attend_body(
    starts_ref, query_ref, grad_ref, both_ref, attended_ref, query_grad_ref, both_grad_ref,
    *, byte_count
):
    shard = lax.axis_index(BYTE)
    shard_total, slot_count = starts_ref.shape
    slot_total = shard_total * slot_count
    heads = query_ref.shape[1] // HS
    factor = 1.0 / math.sqrt(HS)
    used = jnp.sum((starts_ref[...] < byte_count).astype(jnp.int32), axis=1, keepdims=True)
    ids = lax.broadcasted_iota(jnp.int32, (shard_total, slot_total), 1)
    shards = lax.broadcasted_iota(jnp.int32, (shard_total, slot_total), 0)
    inside = ids - shards * slot_count
    usable = jnp.max(
        ((inside >= 0) & (inside < used)).astype(F32), axis=0, keepdims=True
    )
    mine = lax.broadcasted_iota(jnp.int32, (shard_total, 1), 0) == shard
    own_used = jnp.sum(jnp.where(mine, used, 0), axis=0, keepdims=True)
    live = (lax.broadcasted_iota(jnp.int32, (slot_count, 1), 0) < own_used).astype(F32)
    rows = lax.broadcasted_iota(jnp.int32, (slot_count, slot_total), 0) + shard * slot_count
    cols = lax.broadcasted_iota(jnp.int32, (slot_count, slot_total), 1)
    visible = (cols <= rows) & (usable > 0.0)
    keys = both_ref[:, :HS]
    values = both_ref[:, HS:]
    query = stacked(query_ref[...], heads)
    grad = stacked(grad_ref[...], heads)
    live_rows = jnp.concatenate([live] * heads, axis=0)
    seen = jnp.concatenate([visible.astype(F32)] * heads, axis=0) > 0.0
    grad = (grad.astype(F32) * live_rows).astype(BF)
    scores = jnp.where(seen, rows_by_rows(query, keys) * factor, -1e30)
    highest = jnp.max(scores, axis=1, keepdims=True)
    raised = jnp.where(seen, jnp.exp(scores - highest), 0.0)
    total = jnp.maximum(jnp.sum(raised, axis=1, keepdims=True), 1.0)
    attention = raised * (1.0 / total)
    short = attention.astype(BF)
    mixed = rows_by_cols(short, values)
    attended_ref[...] = side_by_side((mixed * live_rows).astype(BF), heads)
    dots = jnp.sum(grad.astype(F32) * mixed, axis=1, keepdims=True)
    prob_grad = rows_by_rows(grad, values)
    score_grad = (attention * ((prob_grad - dots) * factor)).astype(BF)
    query_grad_ref[...] = side_by_side(rows_by_cols(score_grad, keys).astype(BF), heads)
    both_grad_ref[:, :HS] = cols_by_cols(score_grad, query).astype(BF)
    both_grad_ref[:, HS:] = cols_by_cols(short, grad).astype(BF)


def spread_body(parts_ref, pooled_ref, own_ref, other_ref, patch_ref, keep_ref, give_ref):
    both = gathered_sum(parts_ref).astype(BF)
    globs, xs, slots, width = pooled_ref.shape
    weights = ordered(*pair_of(own_ref, other_ref))
    patch = rows_by_rows(both[:, :HS], weights[0]) + rows_by_rows(both[:, HS:], weights[1])
    patch = patch.astype(BF)
    for y in range(globs):
        patch_ref[y] = patch[:, y * width : (y + 1) * width].reshape(xs, slots, width)
    grad = cols_by_cols(features_of(pooled_ref), both)
    keep, give = ordered(grad[:, :HS].astype(BF), grad[:, HS:].astype(BF))
    keep_ref[...] = keep.reshape(keep_ref.shape)
    give_ref[...] = give.reshape(give_ref.shape)


def add_body(left_ref, right_ref, out_ref):
    out_ref[...] = (left_ref[...].astype(F32) + right_ref[...].astype(F32)).astype(BF)


def byte_body(starts_ref, parts_ref, out_ref):
    members = members_of(starts_ref, lax.axis_index(BYTE), out_ref.shape[0])
    counts = counts_of(members)
    globs, xs, slots, width = parts_ref.shape
    pieces = [None] * (xs * width // HS)
    for x in range(xs):
        total = parts_ref[0, x].astype(F32)
        for y in range(1, globs):
            total = total + parts_ref[y, x].astype(F32)
        shared = (total.astype(BF).astype(F32) / counts).astype(BF)
        for half in range(width // HS):
            pieces[half * xs + x] = shared[:, half * HS : (half + 1) * HS]
    out_ref[...] = rows_by_cols(members, jnp.concatenate(pieces, axis=1)).astype(BF)


def on_device(byte_states, patch_start, queries, grad_out, w_kv):
    states = byte_states[0]
    starts = patch_start[0]
    byte_count, width = states.shape
    shard_total, slot_count = starts.shape
    slot_total = shard_total * slot_count
    globs = lax.axis_size("glob")
    depth = lax.axis_size("byte_0")
    across = lax.axis_size("byte_1")
    block = slot_total // depth
    both = 2 * HS
    halves = width // (across * HS)

    swap = [(0, 1), (1, 0)]
    own = exchange(call(copy_body, shape((depth, HS, HS)), w_kv, name="copies"), "byte_0")
    other = lax.ppermute(own, "dp", swap)
    send = call(
        pool_body, shape((globs, across, slot_count, halves * HS)), starts, states, name="pool"
    )
    pooled = exchange(send.reshape(globs * across, slot_count, halves * HS), CROSS)
    pooled = pooled.reshape(globs, across, slot_count, halves * HS)
    send = call(project_body, shape((across, block, both)), pooled, own, other, name="project")
    parts = exchange(send, "byte_1")
    send = call(share_body, shape((depth, block, both)), parts, name="share")
    key_value = exchange(send, "byte_0").reshape(slot_total, both)
    rows = queries.shape[1:]
    attended, query_grad, send = call(
        functools.partial(attend_body, byte_count=byte_count),
        (shape(rows), shape(rows), shape((slot_total, both))),
        starts, queries[0], grad_out[0], key_value,
        name="attend",
    )
    parts = exchange(send.reshape(depth, block, both), "byte_0")
    send = call(share_body, shape((across, block, both)), parts, name="share_grad")
    parts = exchange(send, "byte_1")
    blocks = shape((depth, HS, HS))
    patch_send, keep, give = call(
        spread_body, (shape((globs, across, slot_count, halves * HS)), blocks, blocks),
        parts, pooled, own, other,
        name="spread",
    )
    given = lax.ppermute(give, "dp", swap)
    parts = exchange(patch_send.reshape(globs * across, slot_count, halves * HS), CROSS)
    parts = parts.reshape(globs, across, slot_count, halves * HS)
    byte_grad = call(byte_body, shape((byte_count, width)), starts, parts, name="bytes")
    send = call(add_body, blocks, keep, given, name="sum_dp")
    weight_parts = exchange(send, "byte_0")
    send = call(share_body, shape((2, HS, HS), F32), weight_parts, name="sum_byte")
    pair_grad = exchange(send, "dp")
    return (attended[None], query_grad[None], byte_grad[None], pair_grad)


def solution(mesh):
    torus = Mesh(
        mesh.devices.reshape(mesh.shape["dp"], mesh.shape["glob"], 8, 4),
        ("dp", "glob", "byte_0", "byte_1"),
    )
    in_specs = (
        P("dp", BYTE, "glob"),
        P("dp", None, None),
        P("dp", BYTE, "glob"),
        P("dp", BYTE, "glob"),
        P(None, BYTE, "glob"),
    )
    out_specs = (
        P("dp", BYTE, "glob"),
        P("dp", BYTE, "glob"),
        P("dp", BYTE, "glob"),
        P(None, BYTE, "glob"),
    )
    return jax.shard_map(
        on_device, mesh=torus, in_specs=in_specs, out_specs=out_specs, check_vma=False
    )
```

time: 137 us -> 130 us (0.949)
  blocking collectives: 102 us -> 90.4 us
  starting transfers between devices: 7.56 us -> 14.9 us
  Pallas kernels: 7.63 us -> 5.58 us
    all_to_all x8 -> x7, blocking collectives: 102 us -> 90.4 us  [exchange(): return lax.all_to_all(value, axes, split_axis=0, concat_axis=0, tiled=True)]
    ppermute x0 -> x2, starting transfers between devices: none -> 7.97 us  [the longest x1 5.63 us: on_device(): given = lax.ppermute(give, 'dp', swap)]
    pallas_call x9 -> x10, Pallas kernels: 7.63 us -> 5.58 us  [call(): pl.pallas_call(body, out_shape=outs, in_specs=specs, out_specs=jax.tree.m...]
  transfers between devices with their start and end apart: 2 -> 4, of which waited for: 2 -> 2; matrix products, arithmetic and copies ran while one was open for 0% -> 0% of each run, Pallas kernels for 2% -> 2%
where the time goes in v4:
time: 130 us
  blocking collectives  90.4 us (70%)
  waiting for transfers between devices  16.7 us (13%)
  starting transfers between devices  14.9 us (11%)
  Pallas kernels  5.58 us (4%)
  local copies, waits for them, and re-layouts  1.51 us (1%)
    all_to_all x7, blocking collectives, exchange(): return lax.all_to_all(value, axes, split_axis=0, concat_axis=0, tiled=True)  90.4 us
    all_to_all x2, waiting for transfers between devices, exchange(): return lax.all_to_all(value, axes, split_axis=0, concat_axis=0, tiled=True)  16.6 us
    all_to_all x2, starting transfers between devices, exchange(): return lax.all_to_all(value, axes, split_axis=0, concat_axis=0, tiled=True)  6.94 us
    ppermute x1, starting transfers between devices, on_device(): given = lax.ppermute(give, 'dp', swap)  5.63 us
    pallas_call x10, Pallas kernels, call(): pl.pallas_call(body, out_shape=outs, in_specs=specs, out_specs=jax.tree.m...  5.58 us
  transfers between devices with their start and end apart: 4, of which 2 were waited for; matrix products, arithmetic and copies ran while one was open for 0% of the time, Pallas kernels for 2%

profile of v4, /device:TPU:1, one launch (start us, length us, event | category | flops | bytes accessed | tf_op | source)
XLA Modules:
  0.0 129.8 jit_solution(14153208360680391755)
XLA Ops:
  0.6 0.0 copy-start.2
  0.6 0.8 copy-done.2
  1.5 0.0 copy-start
  1.5 0.0 copy-start.1
  1.5 19.4 %all_to_all.45.own_ref = bf16[8,128,128]{2,1,0:T(8,128)(2,1)S(1)} all-to-all(bf16[8,128,128]{2,1,0:T(8,128)(2,1)S(1)} %copies.1), channel_id=1, replica_groups=mesh['dp'=2,'glob'=4,'byte_0'=8,'byte_1'=4] {'byte_0'}, dimensions={0} | all-to-all | bytes 524288 | tf_op jit(solution)/shard_map/all_to_all | solution.py:20
  21.0 2.3 %collective-permute-start = (bf16[8,128,128]{2,1,0:T(8,128)(2,1)S(1)}, bf16[8,128,128]{2,1,0:T(8,128)(2,1)S(1)}, u32[]{:S(2)}, u32[]{:S(2)}) collective-permute-start(bf16[8,128,128]{2,1,0:T(8,128)(2,1)S(1)} %all_to_all.45.own_ref), channel_id=1, source_target_pairs={{0,128},{128,0},{1,129},{129,1},{2,130},{130,2},{3,131},{131,3},{4... | collective-permute-start | bytes 786440 | tf_op jit(solution)/shard_map/ppermute | solution.py:227
  23.3 0.0 copy-done
  23.3 0.0 copy-done.1
  23.3 0.5 pool.1
  23.8 15.0 %all_to_all.46 = bf16[16,32,256]{2,1,0:T(8,128)(2,1)S(1)} all-to-all(bf16[16,32,256]{2,1,0:T(8,128)(2,1)S(1)} %bitcast.17), channel_id=1, replica_groups=mesh['dp'=2,'glob'=4,'byte_0'=8,'byte_1'=4] {'glob','byte_1'}, dimensions={0} | all-to-all | bytes 524288 | tf_op jit(solution)/shard_map/all_to_all | solution.py:20
  38.8 0.0 collective-permute-done.other_ref
  38.8 0.3 project.1
  39.2 7.9 %all_to_all.47.parts_ref = bf16[4,128,256]{2,1,0:T(8,128)(2,1)S(1)} all-to-all(bf16[4,128,256]{2,1,0:T(8,128)(2,1)S(1)} %project.1), channel_id=1, replica_groups=mesh['dp'=2,'glob'=4,'byte_0'=8,'byte_1'=4] {'byte_1'}, dimensions={0} | all-to-all | bytes 524288 | tf_op jit(solution)/shard_map/all_to_all | solution.py:20
  47.1 0.0 copy-start.3
  47.1 0.0 copy-start.4
  47.1 17.0 %all_to_all.48 = bf16[8,128,256]{2,1,0:T(8,128)(2,1)S(1)} all-to-all(bf16[8,128,256]{2,1,0:T(8,128)(2,1)S(1)} %share.1), channel_id=1, replica_groups=mesh['dp'=2,'glob'=4,'byte_0'=8,'byte_1'=4] {'byte_0'}, dimensions={0} | all-to-all | bytes 1048576 | tf_op jit(solution)/shard_map/all_to_all | solution.py:20
  64.1 0.0 copy-done.3
  64.1 0.0 copy-done.4
  64.1 1.5 %attend.1 = (bf16[32,512]{1,0:T(8,128)(2,1)}, bf16[32,512]{1,0:T(8,128)(2,1)}, bf16[1024,256]{1,0:T(8,128)(2,1)S(1)}) custom-call(s32[32,32]{1,0:T(8,128)S(1)} %bitcast.21, bf16[32,512]{1,0:T(8,128)(2,1)S(1)} %bitcast.23, bf16[32,512]{1,0:T(8,128)(2,1)S(1)} %bitcast.24, bf16[1024,256]{1,0:T(8,128)(2,1)S(1)} %bitcast.15), custom_call_target="tpu_custom_call" | custom-call | tf_op jit(solution)/shard_map/attend/pallas_call | solution.py:41
  65.7 16.6 %all_to_all.49.parts_ref = bf16[8,128,256]{2,1,0:T(8,128)(2,1)S(1)} all-to-all(bf16[8,128,256]{2,1,0:T(8,128)(2,1)S(1)} %bitcast.18), channel_id=1, replica_groups=mesh['dp'=2,'glob'=4,'byte_0'=8,'byte_1'=4] {'byte_0'}, dimensions={0} | all-to-all | bytes 1048576 | tf_op jit(solution)/shard_map/all_to_all | solution.py:20
  82.3 0.1 share_grad.1
  82.3 8.4 %all_to_all.50.parts_ref = bf16[4,128,256]{2,1,0:T(8,128)(2,1)S(1)} all-to-all(bf16[4,128,256]{2,1,0:T(8,128)(2,1)S(1)} %share_grad.1), channel_id=1, replica_groups=mesh['dp'=2,'glob'=4,'byte_0'=8,'byte_1'=4] {'byte_1'}, dimensions={0} | all-to-all | bytes 524288 | tf_op jit(solution)/shard_map/all_to_all | solution.py:20
  90.8 1.0 spread.1
  91.8 5.6 %collective-permute-start.1 = (bf16[8,128,128]{2,1,0:T(8,128)(2,1)S(1)}, bf16[8,128,128]{2,1,0:T(8,128)(2,1)S(1)}, u32[]{:S(2)}, u32[]{:S(2)}) collective-permute-start(bf16[8,128,128]{2,1,0:T(8,128)(2,1)S(1)} %get-tuple-element.15), channel_id=1, source_target_pairs={{0,128},{128,0},{1,129},{129,1},{2,130},{130,2},{3,131},{131,3},{4... | collective-permute-start | bytes 786440 | tf_op jit(solution)/shard_map/ppermute | solution.py:253
  97.4 3.5 %all-to-all-start.6 = ((bf16[16,32,256]{2,1,0:T(8,128)(2,1)}), bf16[16,32,256]{2,1,0:T(8,128)(2,1)S(1)}, u32[]{:S(2)}, u32[]{:S(2)}) async-start(bf16[16,32,256]{2,1,0:T(8,128)(2,1)} %bitcast.10), calls=%async_computation.6 | async-start | bytes 524288 | tf_op jit(solution)/shard_map/all_to_all | solution.py:20
  101.0 0.0 collective-permute-done.1.right_ref
  101.0 0.8 sum_dp.1
  101.7 7.7 %all-to-all-done.6 = bf16[16,32,256]{2,1,0:T(8,128)(2,1)S(1)} async-done(((bf16[16,32,256]{2,1,0:T(8,128)(2,1)}), bf16[16,32,256]{2,1,0:T(8,128)(2,1)S(1)}, u32[]{:S(2)}, u32[]{:S(2)}) %all-to-all-start.6) | async-done | bytes 262176 | tf_op jit(solution)/shard_map/all_to_all | solution.py:20
  109.4 3.4 %all-to-all-start.7 = ((bf16[8,128,128]{2,1,0:T(8,128)(2,1)}), bf16[8,128,128]{2,1,0:T(8,128)(2,1)S(1)}, u32[]{:S(2)}, u32[]{:S(2)}) async-start(bf16[8,128,128]{2,1,0:T(8,128)(2,1)} %sum_dp.1), calls=%async_computation.7 | async-start | bytes 524288 | tf_op jit(solution)/shard_map/all_to_all | solution.py:20
  112.9 1.3 bytes.1
  114.1 8.9 %all-to-all-done.7.parts_ref = bf16[8,128,128]{2,1,0:T(8,128)(2,1)S(1)} async-done(((bf16[8,128,128]{2,1,0:T(8,128)(2,1)}), bf16[8,128,128]{2,1,0:T(8,128)(2,1)S(1)}, u32[]{:S(2)}, u32[]{:S(2)}) %all-to-all-start.7) | async-done | bytes 262176 | tf_op jit(solution)/shard_map/all_to_all | solution.py:20
  123.1 6.0 %all_to_all.51 = f32[2,128,128]{2,1,0:T(8,128)S(1)} all-to-all(f32[2,128,128]{2,1,0:T(8,128)S(1)} %sum_byte.1), channel_id=1, replica_groups=mesh['dp'=2,'glob'=4,'byte_0'=8,'byte_1'=4] {'dp'}, dimensions={0} | all-to-all | bytes 262144 | tf_op jit(solution)/shard_map/all_to_all | solution.py:20
  129.1 0.7 copy.10
  (3 shorter events, 0.1 us)
Async XLA Ops:
  0.6 0.8 copy-start.2
  1.5 21.8 %copy-start = (bf16[1,128,1024]{2,1,0:T(8,128)(2,1)S(1)}, bf16[1,128,1024]{2,1,0:T(8,128)(2,1)}, u32[]{:S(2)}) copy-start(bf16[1,128,1024]{2,1,0:T(8,128)(2,1)} %param.5) | copy-start | bytes 786436
  1.5 21.8 %copy-start.1 = (s32[1,32,32]{2,1,0:T(8,128)S(1)}, s32[1,32,32]{2,1,0:T(8,128)}, u32[]{:S(2)}) copy-start(s32[1,32,32]{2,1,0:T(8,128)} %param.6) | copy-start | bytes 12292
  21.0 17.8 %collective-permute-start = (bf16[8,128,128]{2,1,0:T(8,128)(2,1)S(1)}, bf16[8,128,128]{2,1,0:T(8,128)(2,1)S(1)}, u32[]{:S(2)}, u32[]{:S(2)}) collective-permute-start(bf16[8,128,128]{2,1,0:T(8,128)(2,1)S(1)} %all_to_all.45.own_ref), channel_id=1, source_target_pairs={{0,128},{128,0},{1,129},{129,1},{2,130},{130,2},{3,131},{131,3},{4... | collective-permute-start | bytes 786440 | tf_op jit(solution)/shard_map/ppermute | solution.py:227
  47.1 17.0 %copy-start.3 = (bf16[1,32,512]{2,1,0:T(8,128)(2,1)S(1)}, bf16[1,32,512]{2,1,0:T(8,128)(2,1)}, u32[]{:S(2)}) copy-start(bf16[1,32,512]{2,1,0:T(8,128)(2,1)} %param.7) | copy-start | bytes 98308
  47.1 17.0 %copy-start.4 = (bf16[1,32,512]{2,1,0:T(8,128)(2,1)S(1)}, bf16[1,32,512]{2,1,0:T(8,128)(2,1)}, u32[]{:S(2)}) copy-start(bf16[1,32,512]{2,1,0:T(8,128)(2,1)} %param.8) | copy-start | bytes 98308
  91.8 9.2 %collective-permute-start.1 = (bf16[8,128,128]{2,1,0:T(8,128)(2,1)S(1)}, bf16[8,128,128]{2,1,0:T(8,128)(2,1)S(1)}, u32[]{:S(2)}, u32[]{:S(2)}) collective-permute-start(bf16[8,128,128]{2,1,0:T(8,128)(2,1)S(1)} %get-tuple-element.15), channel_id=1, source_target_pairs={{0,128},{128,0},{1,129},{129,1},{2,130},{130,2},{3,131},{131,3},{4... | collective-permute-start | bytes 786440 | tf_op jit(solution)/shard_map/ppermute | solution.py:253
  97.4 12.0 %all-to-all-start.6 = ((bf16[16,32,256]{2,1,0:T(8,128)(2,1)}), bf16[16,32,256]{2,1,0:T(8,128)(2,1)S(1)}, u32[]{:S(2)}, u32[]{:S(2)}) async-start(bf16[16,32,256]{2,1,0:T(8,128)(2,1)} %bitcast.10), calls=%async_computation.6 | async-start | bytes 524288 | tf_op jit(solution)/shard_map/all_to_all | solution.py:20
  109.4 13.6 %all-to-all-start.7 = ((bf16[8,128,128]{2,1,0:T(8,128)(2,1)}), bf16[8,128,128]{2,1,0:T(8,128)(2,1)S(1)}, u32[]{:S(2)}, u32[]{:S(2)}) async-start(bf16[8,128,128]{2,1,0:T(8,128)(2,1)} %sum_dp.1), calls=%async_computation.7 | async-start | bytes 524288 | tf_op jit(solution)/shard_map/all_to_all | solution.py:20
